TPU v7x, 128 devices: a whole 4x4x4 slice. The times are simulated.
128 devices in a mesh: gx: 4 (over x), gy: 4 (over z), gz: 8 (over y, core).
Axes of the slice: x: 4, y: 4, z: 4, core: 2. Of those that a mesh axis runs over, the one named last changes fastest.
Arguments:
- force: float32 [3, 128, 64, 1024], P(None, 'gx', 'gy', 'gz'), may hold values from -6 to 6
- phase: int32 [128, 64, 1024], P('gx', 'gy', 'gz'), may hold values from 0 to 7
- viscosity_table: float32 [8], replicated, may hold values from 0.1 to 10
- boundary_flags: int32 [6], replicated, may hold values from 0 to 1
Outputs:
- pressure: float32 [128, 64, 1024], P('gx', 'gy', 'gz')
- residual: float32 [128, 64, 1024], P('gx', 'gy', 'gz')
- res_norms: float32 [3], replicated
Inputs may be any that keep to these rules, and one draw needn't show every extreme that they name: phase ids index viscosity_table. `boundary_flags`: 0 marks a no-slip face, 1 a free-slip face.
All inputs are finite; a program needn't handle non-finite values.
Results may differ from a plain program's by a relative error of at most 0.0003.
Values sent between devices are 32-bit elements; how exact they have to be, the bound alone decides.
A program may use at most 192 MiB of HBM per device.

v0:
```python
import functools

import jax
import jax.numpy as jnp
from jax import lax
from jax.experimental import pallas as pl
from jax.experimental.pallas import tpu as pltpu
from jax.sharding import PartitionSpec as P

ITERS = 3
OMEGA = 0.8
F32 = jnp.float32
MESH = pl.DeviceIdType.MESH

BX, BY, BZ = 32, 16, 128
ROWS = BX * BY
G = 24
EROWS = 2 * G + 40 * 24
SROWS = 2 * G + 5 * 24
NSETS = 7

DIRS = [(dx, dy, dz) for dz in (0, 1, -1) for dy in (1, -1, 0) for dx in (0, 1, -1) if (dx, dy, dz) != (0, 0, 0)]
DIRS.sort(key=lambda d: (d[1] == 0 or d[0] != 0 or d[2] != 0, sum(map(abs, d))))
DIR_AT = {d: i for i, d in enumerate(DIRS)}


def piece_rows(d):
    dx, dy, dz = d
    if dz == 0:
        if dx and dy:
            return 16
        return 128 if dy else 80
    if dx and dy:
        return 8
    if dy:
        return 32
    return 16 if dx else 64


OFFSETS = {}
RECV_ROWS = 0
for _d in DIRS:
    OFFSETS[_d] = RECV_ROWS
    RECV_ROWS += piece_rows(_d)


def iota(shape, dim):
    return lax.broadcasted_iota(jnp.int32, shape, dim)


def roll_lanes(v, by):
    by = by % 128
    return v if by == 0 else pltpu.roll(v, by, 1)


def roll_rows(v, by):
    return pltpu.roll(v, by % v.shape[0], 0)


def kernel(
    sizes,
    force_hbm, phase_hbm, table, flags,
    press_out, resid_out, norms_out,
    phase, field, ystage, cstage, dstage, y5, recv, r5,
    ext, slab, kmain, kslab, wmain, wslab, smain, sslab, va, vb, sa, sb, inj,
    res, sch, wap, sim, tim, nap, pre,
    red, red1, red2,
    in_sem, out_sem, send_sem, recv_sem, send5_sem, recv5_sem, rs1, rr1, rs2, rr2,
):
    nx, ny, nz = sizes
    at = (lax.axis_index("gx"), lax.axis_index("gy"), lax.axis_index("gz"))

    def neighbour(d):
        ok = None
        for dim in range(3):
            if d[dim] == 0:
                continue
            here = at[dim] < sizes[dim] - 1 if d[dim] > 0 else at[dim] > 0
            ok = here if ok is None else jnp.logical_and(ok, here)
        return ok, tuple(at[dim] + d[dim] for dim in range(3))

    def recv_at(k, d, start=0, rows=None):
        return recv.at[k, pl.ds(OFFSETS[d] + start, piece_rows(d) if rows is None else rows)]

    def pieces(k, d):
        dx, dy, dz = d
        to = tuple(-a for a in d)
        if dz == 0:
            if dx and dy:
                side = 0 if dy < 0 else 1
                src = ystage.at[k, side, pl.ds(0 if dx < 0 else 112, 16)]
                return src, recv_at(k, to)
            if dy:
                return ystage.at[k, 0 if dy < 0 else 1], recv_at(k, to)
            if dx < 0:
                return field.at[k, pl.ds(0, 64)], recv_at(k, to, 0, 64)
            if isinstance(k, int) and k == 0:
                return field.at[k, pl.ds(ROWS - 80, 80)], recv_at(k, to)
            return field.at[k, pl.ds(ROWS - 64, 64)], recv_at(k, to, 16, 64)
        if dx and dy:
            return dstage.at[k, pl.ds(0 if dx < 0 else 24, 8)], recv_at(k, to)
        if dy:
            return dstage.at[k], recv_at(k, to)
        if dx:
            return cstage.at[k, pl.ds(0 if dx < 0 else 48, 16)], recv_at(k, to)
        return cstage.at[k], recv_at(k, to)

    def copy_of(k, d):
        src, dst = pieces(k, d)
        _, device = neighbour(d)
        to = tuple(-a for a in d)
        return pltpu.make_async_remote_copy(
            src_ref=src, dst_ref=dst,
            send_sem=send_sem.at[k, DIR_AT[d]], recv_sem=recv_sem.at[k, DIR_AT[to]],
            device_id=device, device_id_type=MESH,
        )

    def incoming(k, d):
        to = tuple(-a for a in d)
        src, dst = pieces(k, to)
        return pltpu.make_async_remote_copy(
            src_ref=src, dst_ref=dst,
            send_sem=send_sem.at[k, DIR_AT[to]], recv_sem=recv_sem.at[k, DIR_AT[d]],
            device_id=at, device_id_type=MESH,
        )

    sub8 = iota((8, 128), 0)
    lane8 = iota((8, 128), 1)
    group8, slot8 = lane8 // 16, lane8 % 16
    lane24 = iota((24, 128), 1)
    sub24 = iota((24, 128), 0)
    group24, slot24 = lane24 // 16, lane24 % 16


    def pack(k):
        def pair(xp, _):
            base = pl.multiple_of(xp * 32, 32)
            a0, a1 = field[k, pl.ds(base, 8), :], field[k, pl.ds(base + 8, 8), :]
            b0, b1 = field[k, pl.ds(base + 16, 8), :], field[k, pl.ds(base + 24, 8), :]
            to = pl.multiple_of(xp * 8, 8)
            ystage[k, 0, pl.ds(to, 8), :] = jnp.where(sub8 < 4, a0, roll_rows(b0, 4))
            ystage[k, 1, pl.ds(to, 8), :] = jnp.where(sub8 < 4, roll_rows(a1, 4), b1)
            return 0
        lax.fori_loop(0, BX // 2, pair, 0, unroll=8)

        def block(xb, _):
            acc = [[jnp.zeros((8, 128), F32) for _ in range(2)] for _ in range(3)]
            for g in range(8):
                base = pl.multiple_of(xb * 128, 128) + g * 16
                a, b = field[k, pl.ds(base, 8), :], field[k, pl.ds(base + 8, 8), :]
                for i, v in enumerate((a, b, jnp.where(sub8 < 4, a, b))):
                    acc[i][0] = jnp.where(group8 == g, roll_lanes(v, 5 + 16 * g), acc[i][0])
                    acc[i][1] = jnp.where(group8 == g, roll_lanes(v, 12 + 16 * g), acc[i][1])
            a, b, c = (jnp.where(slot8 < 9, u, v) for u, v in acc)
            to = pl.multiple_of(xb * 16, 16)
            cstage[k, pl.ds(to, 8), :] = a
            cstage[k, pl.ds(to + 8, 8), :] = b
            dstage[k, pl.ds(pl.multiple_of(xb * 8, 8), 8), :] = c
            return 0
        lax.fori_loop(0, 4, block, 0, unroll=2)

    def send(k):
        for d in DIRS:
            ok, _ = neighbour(d)

            @pl.when(ok)
            def _():
                copy_of(k, d).start()

    def receive(k):
        for d in DIRS:
            ok, _ = neighbour(d)

            @pl.when(ok)
            def _():
                incoming(k, d).wait_recv()

    def finish_sends(k):
        for d in DIRS:
            ok, _ = neighbour(d)

            @pl.when(ok)
            def _():
                copy_of(k, d).wait_send()

    def unpack(k):
        def planes(own, low, high, first, pairs):
            def pair(xp, _):
                src = pl.multiple_of(xp * 32, 32)
                side = pl.multiple_of(xp * 8, 8)
                lo, hi = low(side), high(side)
                los, his = roll_rows(lo, 4), roll_rows(hi, 4)
                for half in range(2):
                    ra, rb = roll_rows(own(src + 16 * half), 4), roll_rows(own(src + 16 * half + 8), 4)
                    to = pl.multiple_of(xp * 48, 8) + (G + (first + half) * 24)
                    ext[pl.ds(to, 8), :] = jnp.where(sub8 < 4, (lo, los)[half], ra)
                    ext[pl.ds(to + 8, 8), :] = jnp.where(sub8 < 4, ra, rb)
                    ext[pl.ds(to + 16, 8), :] = jnp.where(sub8 < 4, rb, (his, hi)[half])
                return 0
            lax.fori_loop(0, pairs, pair, 0, unroll=min(pairs, 4))

        def of(d, start=0):
            return lambda at_row: recv[k, pl.ds(at_row + (OFFSETS[d] + start), 8), :]

        planes(lambda r: field[k, pl.ds(r, 8), :], of((0, -1, 0)), of((0, 1, 0)), 4, 16)
        planes(of((-1, 0, 0), 16), of((-1, -1, 0)), of((-1, 1, 0)), 0, 2)
        planes(of((1, 0, 0)), of((1, -1, 0)), of((1, 1, 0)), 36, 2)

        def merged(d, row):
            low = recv[k, pl.ds(OFFSETS[(d[0], d[1], -1)] + row, 8), :]
            high = recv[k, pl.ds(OFFSETS[(d[0], d[1], 1)] + row, 8), :]
            return jnp.where(slot8 < 8, low, high)

        inner = []
        for t in range(2):
            inner.append([merged((-1, 0), 8 * t)] + [merged((0, 0), xb * 16 + 8 * t) for xb in range(4)] + [merged((1, 0), 8 * t)])
        sides = []
        for xb in range(6):
            dx, row = (-1, 0) if xb == 0 else (1, 0) if xb == 5 else (0, (xb - 1) * 8)
            sides.append(roll_rows(jnp.where(sub8 < 4, merged((dx, 1), row), merged((dx, -1), row)), 4))

        def shifted(parts, i):
            return roll_lanes(jnp.where(group8 < 4, parts[i + 1], parts[i]), 64)

        for i in range(5):
            a, b = roll_rows(shifted(inner[0], i), 4), roll_rows(shifted(inner[1], i), 4)
            c = shifted(sides, i)
            tiles = (jnp.where(sub8 < 4, c, a), jnp.where(sub8 < 4, a, b), jnp.where(sub8 < 4, b, c))
            for t in range(3):
                slab[pl.ds(G + i * 24 + 8 * t, 8), :] = tiles[t]

        def own(i, _):
            base = pl.multiple_of(i * 192, 8) + G
            to = pl.multiple_of(i * 24, 8) + G
            for t in range(3):
                lo, hi = jnp.zeros((8, 128), F32), jnp.zeros((8, 128), F32)
                for j in range(8):
                    v = ext[pl.ds(base + j * 24 + 8 * t, 8), :]
                    lo = jnp.where(group8 == j, roll_lanes(v, 5 + 16 * j), lo)
                    hi = jnp.where(group8 == j, roll_lanes(v, 12 + 16 * j), hi)
                mine = jnp.where(slot8 < 9, lo, hi)
                old = slab[pl.ds(to + 8 * t, 8), :]
                slab[pl.ds(to + 8 * t, 8), :] = jnp.where((slot8 >= 5) & (slot8 < 12), mine, old)
            return 0
        lax.fori_loop(0, 5, own, 0)


    def make_injection(source, c, rows0, out):
        v = source[c, pl.ds(rows0, 24), :]
        out[c, pl.ds(rows0, 24), :] = jnp.where(slot24 == 5, roll_lanes(v, -7), v)

    def main_z(v, c, i, j):
        edge = roll_lanes(inj[c, pl.ds(pl.multiple_of(i * 24, 8) + G, 24), :], 123 - 16 * j)
        up = roll_lanes(jnp.where(lane24 == 0, edge, v), 127)
        down = roll_lanes(jnp.where(lane24 == 127, edge, v), 1)
        return up, down

    def slab_x(v, below, above):
        up = roll_lanes(jnp.where(lane24 < 16, above, v), -16)
        down = roll_lanes(jnp.where(lane24 >= 112, below, v), 16)
        return up, down

    def for_planes(first, last, body):
        for p in range(first, 8):
            body(0, p)

        def block(i, _):
            for j in range(8):
                body(i, j)
            return 0
        lax.fori_loop(1, 4, block, 0)
        for p in range(32, last + 1):
            body(4, p - 32)

    def row_of(i, j):
        return pl.multiple_of(i * 192, 8) + (G + j * 24)

    def shift_rows(ref, c, base, by):
        return ref[c, pl.ds(base + by, 24), :]


    walls = [jnp.where(flags[f] == 0, F32(1.0), F32(0.0)) for f in range(6)]
    totals = (nx * BX, ny * BY, nz * BZ)

    def coefficients(e, nbrs, spots):
        faces = []
        inside = None
        diag = jnp.zeros_like(e)
        extra = [jnp.zeros_like(e) for _ in range(3)]
        for axis in range(3):
            for side in range(2):
                spot = spots[axis] + (1 if side else -1)
                here = (spot >= 0) & (spot < totals[axis])
                face = 0.5 * (e + nbrs[axis][side])
                wall = walls[2 * axis + side]
                outer = jnp.where(here, F32(0.0), e)
                diag = diag + jnp.where(here, face, e * wall)
                extra[axis] = extra[axis] + outer * (1.0 - wall)
                faces.append(face)
            here = (spots[axis] >= 0) & (spots[axis] < totals[axis])
            inside = here if inside is None else inside & here
        weights = []
        for c in range(3):
            d = diag + extra[c]
            good = inside & (d > 0)
            weights.append(jnp.where(good, OMEGA / jnp.where(good, d, F32(1.0)), F32(0.0)))
        return faces, weights

    def setup():
        for t in range(2):
            v = roll_rows(recv[0, pl.ds(OFFSETS[(-1, 0, 0)] + 8 * t, 8), :], 4)
            if t == 0:
                ext[pl.ds(0, 8), :] = jnp.where(sub8 < 4, F32(0.0), v)
                keep = v
            else:
                ext[pl.ds(8, 8), :] = jnp.where(sub8 < 4, keep, v)
                ext[pl.ds(16, 8), :] = jnp.where(sub8 < 4, v, F32(0.0))

        def injection(i, _):
            base = pl.multiple_of(i * 24, 8) + G
            v = slab[pl.ds(base, 24), :]
            inj[0, pl.ds(base, 24), :] = jnp.where(slot24 == 5, roll_lanes(v, -7), v)
            return 0
        lax.fori_loop(0, 5, injection, 0)

        def main_block(i, _):
            fives = roll_rows(jnp.where(sub8 < 4, r5[pl.ds(pl.multiple_of(i * 8, 8) + 8, 8), :], r5[pl.ds(pl.multiple_of(i * 8, 8), 8), :]), 4)
            for j in range(8):
                b = row_of(i, j)
                e = ext[pl.ds(b, 24), :]
                up, down = main_z(e, 0, i, j)
                five = jnp.broadcast_to(fives[j:j + 1, :], (24, 128))
                below = jnp.where(sub24 == 0, five, ext[pl.ds(b - 1, 24), :])
                nbrs = (
                    (ext[pl.ds(b - 24, 24), :], ext[pl.ds(b + 24, 24), :]),
                    (below, ext[pl.ds(b + 1, 24), :]),
                    (down, up),
                )
                spots = (
                    jnp.broadcast_to(at[0] * BX + (i * 8 + j - 4), (24, 128)),
                    sub24 + (at[1] * BY - 4),
                    lane24 + at[2] * BZ,
                )
                faces, weights = coefficients(e, nbrs, spots)
                for f in range(6):
                    kmain[f, pl.ds(b, 24), :] = faces[f]
                for c in range(3):
                    wmain[c, pl.ds(b, 24), :] = weights[c]
            return 0
        lax.fori_loop(0, 5, main_block, 0)

        def slab_block(i, _):
            b = pl.multiple_of(i * 24, 8) + G
            e = slab[pl.ds(b, 24), :]
            xu, xd = slab_x(e, slab[pl.ds(b - 24, 24), :], slab[pl.ds(b + 24, 24), :])
            nbrs = (
                (xd, xu),
                (slab[pl.ds(b - 1, 24), :], slab[pl.ds(b + 1, 24), :]),
                (roll_lanes(e, 1), roll_lanes(e, 127)),
            )
            spots = (
                group24 + (at[0] * BX - 4 + i * 8),
                sub24 + (at[1] * BY - 4),
                jnp.where(slot24 < 9, slot24 - 5, slot24 + 116) + at[2] * BZ,
            )
            faces, weights = coefficients(e, nbrs, spots)
            for f in range(6):
                kslab[f, pl.ds(b, 24), :] = faces[f]
            for c in range(3):
                wslab[c, pl.ds(b, 24), :] = weights[c]
            return 0
        lax.fori_loop(0, 5, slab_block, 0)


    def gradient():
        def slab_block(i, _):
            b = pl.multiple_of(i * 24, 8) + G
            p = slab[pl.ds(b, 24), :]
            above = slab[pl.ds(b + 24, 24), :]
            xu = roll_lanes(jnp.where(lane24 < 16, above, p), -16)
            nbrs = (xu, slab[pl.ds(b + 1, 24), :], roll_lanes(p, 127))
            for c in range(3):
                sslab[c, pl.ds(b, 24), :] = wslab[c, pl.ds(b, 24), :] * (nbrs[c] - p)
            inj[0, pl.ds(b, 24), :] = jnp.where(slot24 == 5, roll_lanes(p, -7), p)
            return 0
        lax.fori_loop(0, 5, slab_block, 0)

        def plane(i, j):
            b = row_of(i, j)
            p = ext[pl.ds(b, 24), :]
            edge = roll_lanes(inj[0, pl.ds(pl.multiple_of(i * 24, 8) + G, 24), :], 123 - 16 * j)
            zu = roll_lanes(jnp.where(lane24 == 0, edge, p), 127)
            nbrs = (ext[pl.ds(b + 24, 24), :], ext[pl.ds(b + 1, 24), :], zu)
            for c in range(3):
                smain[c, pl.ds(b, 24), :] = wmain[c, pl.ds(b, 24), :] * (nbrs[c] - p)
        for_planes(0, 38, plane)

    def scaled_force(c):
        def slab_block(i, _):
            b = pl.multiple_of(i * 24, 8) + G
            sslab[c, pl.ds(b, 24), :] = wslab[c, pl.ds(b, 24), :] * slab[pl.ds(b, 24), :]
            return 0
        lax.fori_loop(0, 5, slab_block, 0)

        def block(i, _):
            for j in range(8):
                b = row_of(i, j)
                smain[c, pl.ds(b, 24), :] = wmain[c, pl.ds(b, 24), :] * ext[pl.ds(b, 24), :]
            return 0
        lax.fori_loop(0, 5, block, 0)

    def injections(source):
        def block(i, _):
            b = pl.multiple_of(i * 24, 8) + G
            for c in range(3):
                make_injection(source, c, b, inj)
            return 0
        lax.fori_loop(0, 5, block, 0, unroll=True)

    def sweep(src, dst, ssrc, sdst, first, last, with_slab):
        injections(ssrc)

        def plane(i, j):
            b = row_of(i, j)
            k = [kmain[f, pl.ds(b, 24), :] for f in range(6)]
            for c in range(3):
                v = src[c, pl.ds(b, 24), :]
                zu, zd = main_z(v, c, i, j)
                total = k[0] * src[c, pl.ds(b - 24, 24), :] + k[1] * src[c, pl.ds(b + 24, 24), :]
                total = total + (k[2] * shift_rows(src, c, b, -1) + k[3] * shift_rows(src, c, b, 1))
                total = total + (k[4] * zd + k[5] * zu)
                dst[c, pl.ds(b, 24), :] = (
                    (1.0 - OMEGA) * v + smain[c, pl.ds(b, 24), :] + wmain[c, pl.ds(b, 24), :] * total
                )
        for_planes(first, last, plane)

        def block(i, _):
            b = pl.multiple_of(i * 24, 8) + G
            k = [kslab[f, pl.ds(b, 24), :] for f in range(6)]
            for c in range(3):
                v = ssrc[c, pl.ds(b, 24), :]
                xu, xd = slab_x(v, ssrc[c, pl.ds(b - 24, 24), :], ssrc[c, pl.ds(b + 24, 24), :])
                total = k[0] * xd + k[1] * xu
                total = total + (k[2] * shift_rows(ssrc, c, b, -1) + k[3] * shift_rows(ssrc, c, b, 1))
                total = total + (k[4] * roll_lanes(v, 1) + k[5] * roll_lanes(v, 127))
                sdst[c, pl.ds(b, 24), :] = (
                    (1.0 - OMEGA) * v + sslab[c, pl.ds(b, 24), :] + wslab[c, pl.ds(b, 24), :] * total
                )
            return 0
        lax.fori_loop(0, 5, block, 0, unroll=True)

    def divergence(src, ssrc, out):
        def block(i, _):
            b = pl.multiple_of(i * 24, 8) + G
            make_injection(ssrc, 2, b, inj)
            return 0
        lax.fori_loop(0, 5, block, 0, unroll=True)

        def plane(i, j):
            b = row_of(i, j) + 4
            x, y, z = (src[c, pl.ds(b, 16), :] for c in range(3))
            edge = roll_lanes(inj[2, pl.ds(pl.multiple_of(i * 24, 8) + (G + 4), 16), :], 123 - 16 * j)
            zd = roll_lanes(jnp.where(iota((16, 128), 1) == 127, edge, z), 1)
            total = (src[0, pl.ds(b - 24, 16), :] - x) + (src[1, pl.ds(b - 1, 16), :] - y) + (zd - z)
            to = pl.multiple_of(i * 128, 16) + (j * 16 - 64)
            out[pl.ds(to, 16), :] = total
        for_planes(4, 35, plane)

    def apply(out):
        sweep(smain, va, sslab, sa, 1, 37, True)
        sweep(va, vb, sa, sb, 2, 36, True)
        sweep(vb, va, sb, sa, 3, 35, True)
        divergence(va, sa, out)


    me_z = at[2]
    me_xy = at[0] * ny + at[1]
    nxy = nx * ny

    def z_copy(k, off):
        other = lax.rem(me_z + off, nz)
        return pltpu.make_async_remote_copy(
            src_ref=red.at[k], dst_ref=red1.at[k, me_z], send_sem=rs1.at[k, off], recv_sem=rr1.at[k, off],
            device_id=(at[0], at[1], other), device_id_type=MESH,
        )

    def xy_copy(k, ox, oy):
        off = ox * ny + oy
        return pltpu.make_async_remote_copy(
            src_ref=red.at[k], dst_ref=red2.at[k, me_xy], send_sem=rs2.at[k, off], recv_sem=rr2.at[k, off],
            device_id=(lax.rem(at[0] + ox, nx), lax.rem(at[1] + oy, ny), at[2]), device_id_type=MESH,
        )

    offsets_xy = [(ox, oy) for ox in range(nx) for oy in range(ny) if (ox, oy) != (0, 0)]

    def reduce_start(k, value):
        red[k] = value
        red1[k, me_z] = value
        for off in range(1, nz):
            z_copy(k, off).start()

    def reduce_middle(k):
        for off in range(1, nz):
            z_copy(k, off).wait_recv()
        for off in range(1, nz):
            z_copy(k, off).wait_send()
        value = red1[k, 0]
        for i in range(1, nz):
            value = value + red1[k, i]
        red[k] = value
        red2[k, me_xy] = value
        for ox, oy in offsets_xy:
            xy_copy(k, ox, oy).start()

    def reduce_end(k):
        for ox, oy in offsets_xy:
            xy_copy(k, ox, oy).wait_recv()
        for ox, oy in offsets_xy:
            xy_copy(k, ox, oy).wait_send()
        value = red2[k, 0]
        for i in range(1, nxy):
            value = value + red2[k, i]
        value = jnp.broadcast_to(jnp.sum(value, axis=1, keepdims=True), (8, 128))
        return [jnp.broadcast_to(value[i:i + 1, :], (8, 128)) for i in range(3)]


    load_phase = pltpu.make_async_copy(phase_hbm, phase, in_sem.at[0])
    load_force = pltpu.make_async_copy(force_hbm, field.at[pl.ds(1, 3)], in_sem.at[1])
    load_phase.start()
    load_force.start()

    def clear_recv(i, _):
        for k in range(NSETS):
            recv[k, pl.ds(pl.multiple_of(i * 8, 8), 8), :] = jnp.zeros((8, 128), F32)
        return 0
    lax.fori_loop(0, RECV_ROWS // 8, clear_recv, 0, unroll=2)

    for t in range(0, 48, 8):
        r5[pl.ds(t, 8), :] = jnp.zeros((8, 128), F32)

    barrier = pltpu.get_barrier_semaphore()
    count = jnp.int32(0)
    for d in DIRS:
        ok, device = neighbour(d)

        @pl.when(ok)
        def _():
            pl.semaphore_signal(barrier, inc=1, device_id=device, device_id_type=MESH)
        count = count + ok.astype(jnp.int32)
    for off in range(1, nz):
        pl.semaphore_signal(barrier, inc=1, device_id=(at[0], at[1], lax.rem(me_z + off, nz)), device_id_type=MESH)
    for ox, oy in offsets_xy:
        pl.semaphore_signal(
            barrier, inc=1, device_id=(lax.rem(at[0] + ox, nx), lax.rem(at[1] + oy, ny), at[2]), device_id_type=MESH
        )
    count = count + (nz - 1 + nxy - 1)

    zero24 = jnp.zeros((24, 128), F32)
    for ref, rows in ((ext, EROWS), (slab, SROWS)):
        ref[pl.ds(0, 24), :] = zero24
        ref[pl.ds(rows - 24, 24), :] = zero24
    for ref, rows in ((smain, EROWS), (va, EROWS), (vb, EROWS), (sslab, SROWS), (sa, SROWS), (sb, SROWS)):
        for c in range(3):
            ref[c, pl.ds(0, 24), :] = zero24
            ref[c, pl.ds(rows - 24, 24), :] = zero24
    for ref in (smain, va, vb):
        for c in range(3):
            for xx in (0, 1, 2, 37, 38, 39):
                ref[c, pl.ds(G + xx * 24, 24), :] = zero24

    load_phase.wait()

    def lookup(i, _):
        for u in range(4):
            r = pl.multiple_of(i * 32, 32) + 8 * u
            ids = phase[pl.ds(r, 8), :]
            eta = jnp.zeros((8, 128), F32)
            for level in range(8):
                eta = eta + jnp.where(ids == level, table[level], F32(0.0))
            field[0, pl.ds(r, 8), :] = eta
        return 0
    lax.fori_loop(0, ROWS // 32, lookup, 0)
    pack(0)
    for x in range(BX):
        y5[pl.ds(x, 1), :] = field[0, pl.ds(x * 16 + 11, 1), :]
    pl.semaphore_wait(barrier, count)
    send(0)
    has_y_up, _ = neighbour((0, 1, 0))
    has_y_down, _ = neighbour((0, -1, 0))
    copy5_out = pltpu.make_async_remote_copy(
        src_ref=y5, dst_ref=r5.at[pl.ds(8, 32)], send_sem=send5_sem, recv_sem=recv5_sem,
        device_id=(at[0], at[1] + 1, at[2]), device_id_type=MESH,
    )

    @pl.when(has_y_up)
    def _():
        copy5_out.start()
    load_force.wait()

    def send_force(k, _):
        pack(k)
        send(k)
        return 0
    lax.fori_loop(1, 4, send_force, 0)
    receive(0)

    @pl.when(has_y_down)
    def _():
        copy5_out.wait_recv()
    unpack(0)
    setup()

    def take_force(k, _):
        receive(k)
        unpack(k)
        scaled_force(k - 1)
        return 0
    lax.fori_loop(1, 4, take_force, 0)
    apply(res)

    def rows_loop(body, init, step=4):
        def block(i, carry):
            for u in range(step):
                carry = body(pl.multiple_of(i * (8 * step), 8 * step) + 8 * u, carry)
            return carry
        return lax.fori_loop(0, ROWS // (8 * step), block, init)

    def first(r, _):
        field[4, pl.ds(r, 8), :] = field[0, pl.ds(r, 8), :] * res[pl.ds(r, 8), :]
        return 0
    rows_loop(first, 0)

    def schur(k, out):
        receive(k)
        unpack(k)
        gradient()
        apply(out)

    pack(4)
    send(4)
    schur(4, wap)

    zero8 = jnp.zeros((8, 128), F32)

    def partials(gamma, delta, squares):
        sums = [jnp.broadcast_to(jnp.sum(v, axis=0, keepdims=True), (8, 128)) for v in (gamma, delta, squares)]
        return jnp.where(sub8 == 0, sums[0], jnp.where(sub8 == 1, sums[1], jnp.where(sub8 == 2, sums[2], F32(0.0))))

    def start0(r, carry):
        rr, w, e = (ref[pl.ds(r, 8), :] for ref in (res, wap, field.at[0]))
        z = e * rr
        field[5, pl.ds(r, 8), :] = e * w
        return carry[0] + rr * z, carry[1] + w * z, carry[2] + rr * rr
    sums = rows_loop(start0, (zero8, zero8, zero8))
    pack(5)
    send(5)
    reduce_start(0, partials(*sums))
    receive(5)
    reduce_middle(0)
    unpack(5)
    gradient()
    apply(nap)
    gamma, delta, squares = reduce_end(0)
    cells = float(totals[0] * totals[1] * totals[2])
    norms = [squares / cells]
    alpha = gamma / delta

    def step0(r, carry):
        at_r = pl.ds(r, 8)
        e, rr, w, n = field[0, at_r, :], res[at_r, :], wap[at_r, :], nap[at_r, :]
        p = e * rr
        sch[at_r, :] = p
        sim[at_r, :] = w
        tim[at_r, :] = n
        pre[at_r, :] = alpha * p
        rr = rr - alpha * w
        w = w - alpha * n
        res[at_r, :] = rr
        wap[at_r, :] = w
        z = e * rr
        field[6, at_r, :] = e * w
        return carry[0] + rr * z, carry[1] + w * z, carry[2] + rr * rr
    sums = rows_loop(step0, (zero8, zero8, zero8))
    pack(6)
    send(6)
    reduce_start(1, partials(*sums))
    receive(6)
    reduce_middle(1)
    unpack(6)
    gradient()
    apply(nap)
    gamma_old, alpha_old = gamma, alpha
    gamma, delta, squares = reduce_end(1)
    norms.append(squares / cells)
    beta = gamma / gamma_old
    alpha = gamma / (delta - beta * gamma / alpha_old)

    def step1(r, carry):
        at_r = pl.ds(r, 8)
        e, rr, w, n = field[0, at_r, :], res[at_r, :], wap[at_r, :], nap[at_r, :]
        p = e * rr + beta * sch[at_r, :]
        s = w + beta * sim[at_r, :]
        t = n + beta * tim[at_r, :]
        sch[at_r, :] = p
        sim[at_r, :] = s
        pre[at_r, :] = pre[at_r, :] + alpha * p
        rr = rr - alpha * s
        w = w - alpha * t
        res[at_r, :] = rr
        wap[at_r, :] = w
        z = e * rr
        return carry[0] + rr * z, carry[1] + w * z, carry[2] + rr * rr
    sums = rows_loop(step1, (zero8, zero8, zero8))
    reduce_start(2, partials(*sums))
    reduce_middle(2)
    gamma_old, alpha_old = gamma, alpha
    gamma, delta, squares = reduce_end(2)
    norms.append(squares / cells)
    beta = gamma / gamma_old
    alpha = gamma / (delta - beta * gamma / alpha_old)

    def step2(r, _):
        at_r = pl.ds(r, 8)
        rr = res[at_r, :]
        p = field[0, at_r, :] * rr + beta * sch[at_r, :]
        s = wap[at_r, :] + beta * sim[at_r, :]
        pre[at_r, :] = pre[at_r, :] + alpha * p
        res[at_r, :] = rr - alpha * s
        return 0
    rows_loop(step2, 0)
    store_press = pltpu.make_async_copy(pre, press_out, out_sem.at[0])
    store_resid = pltpu.make_async_copy(res, resid_out, out_sem.at[1])
    store_press.start()
    store_resid.start()
    norms_out[...] = jnp.where(lane8 == 0, norms[0], jnp.where(lane8 == 1, norms[1], norms[2]))

    for k in range(NSETS):
        finish_sends(k)

    @pl.when(has_y_up)
    def _():
        copy5_out.wait_send()
    store_press.wait()
    store_resid.wait()


def solution(mesh):
    sizes = (mesh.shape["gx"], mesh.shape["gy"], mesh.shape["gz"])
    nx, ny, nz = sizes

    def per_device(force, phase, table, flags):
        v = functools.partial(pltpu.VMEM)
        dma = pltpu.SemaphoreType.DMA
        scratch = [
            v((ROWS, 128), jnp.int32),
            v((NSETS, ROWS, 128), F32),
            v((NSETS, 2, 128, 128), F32),
            v((NSETS, 64, 128), F32),
            v((NSETS, 32, 128), F32),
            v((32, 128), F32),
            v((NSETS, RECV_ROWS, 128), F32),
            v((48, 128), F32),
            v((EROWS, 128), F32), v((SROWS, 128), F32),
            v((6, EROWS, 128), F32), v((6, SROWS, 128), F32),
            v((3, EROWS, 128), F32), v((3, SROWS, 128), F32),
            v((3, EROWS, 128), F32), v((3, SROWS, 128), F32),
            v((3, EROWS, 128), F32), v((3, EROWS, 128), F32),
            v((3, SROWS, 128), F32), v((3, SROWS, 128), F32),
            v((3, SROWS, 128), F32),
            *[v((ROWS, 128), F32) for _ in range(7)],
            v((ITERS, 8, 128), F32), v((ITERS, nz, 8, 128), F32), v((ITERS, nx * ny, 8, 128), F32),
            dma((2,)), dma((2,)), dma((NSETS, 26)), dma((NSETS, 26)), dma, dma,
            dma((ITERS, nz)), dma((ITERS, nz)), dma((ITERS, nx * ny)), dma((ITERS, nx * ny)),
        ]
        hbm = pl.BlockSpec(memory_space=pl.ANY)
        smem = pl.BlockSpec(memory_space=pltpu.SMEM)
        press, resid, norms = pl.pallas_call(
            functools.partial(kernel, sizes),
            out_shape=(
                jax.ShapeDtypeStruct((ROWS, 128), F32),
                jax.ShapeDtypeStruct((ROWS, 128), F32),
                jax.ShapeDtypeStruct((8, 128), F32),
            ),
            in_specs=[hbm, hbm, smem, smem],
            out_specs=(hbm, hbm, pl.BlockSpec(memory_space=pltpu.VMEM)),
            scratch_shapes=scratch,
            compiler_params=pltpu.CompilerParams(
                collective_id=0, has_side_effects=True, vmem_limit_bytes=60 * 1024 * 1024
            ),
        )(force.reshape(3, ROWS, BZ), phase.reshape(ROWS, BZ), table, flags)
        return press.reshape(BX, BY, BZ), resid.reshape(BX, BY, BZ), norms[0, :ITERS]

    return jax.shard_map(
        per_device,
        mesh=mesh,
        in_specs=(P(None, "gx", "gy", "gz"), P("gx", "gy", "gz"), P(), P()),
        out_specs=(P("gx", "gy", "gz"), P("gx", "gy", "gz"), P()),
        check_vma=False,
    )
```

profile of v0, /device:TPU:1, one launch (start us, length us, event | category | flops | bytes accessed | tf_op | source)
XLA Modules:
  0.0 121.4 jit_solution(14804426234744462085)
XLA Ops:
  0.6 117.2 %shard_map.67 = (f32[512,128]{1,0:T(8,128)}, f32[512,128]{1,0:T(8,128)}, f32[8,128]{1,0:T(8,128)}) custom-call(f32[3,512,128]{2,1,0:T(8,128)} %bitcast.6, s32[512,128]{1,0:T(8,128)} %bitcast.7, f32[8]{0:T(128)} %table.1, s32[6]{0:T(128)} %flags.1), custom_call_target="tpu_custom_call" | custom-call | tf_op jit(solution)/shard_map/pallas_call | solution.py:777
  117.8 1.2 slice_bitcast_fusion
  119.0 0.0 copy-start
  119.0 1.7 %copy.9 = f32[32,16,128]{2,1,0:T(8,128)} copy(f32[32,16,128]{2,1,0:T(8,128)} %bitcast.9) | data formatting | bytes 524288
  120.7 0.0 copy-done
  120.7 0.7 copy.10
Async XLA Ops:
  119.0 1.7 %copy-start = (f32[512,128]{1,0:T(8,128)S(1)}, f32[512,128]{1,0:T(8,128)}, u32[]{:S(2)}) copy-start(f32[512,128]{1,0:T(8,128)} %get-tuple-element.7) | copy-start | bytes 786436
where the time goes:
time: 122 us; the launch traced here: 121 us
  Pallas kernels  117 us (96%)
  local copies, waits for them, and re-layouts  3.61 us (3%)
    pallas_call x1, Pallas kernels, per_device(): pl.pallas_call(functools.partial(kernel, sizes), out_shape=(jax.ShapeDtyp...  117 us

commit v1 on v0

--- a/solution.py
+++ b/solution.py
@@ -62,7 +62,7 @@
     force_hbm, phase_hbm, table, flags,
     press_out, resid_out, norms_out,
     phase, field, ystage, cstage, dstage, y5, recv, r5,
-    ext, slab, kmain, kslab, wmain, wslab, smain, sslab, va, vb, sa, sb, inj,
+    ext, slab, kmain, kslab, wmain, wslab, smain, sslab, va, vb, sa, sb, inj, edge,
     res, sch, wap, sim, tim, nap, pre,
     red, red1, red2,
     in_sem, out_sem, send_sem, recv_sem, send5_sem, recv5_sem, rs1, rr1, rs2, rr2,
@@ -249,10 +249,17 @@
         v = source[c, pl.ds(rows0, 24), :]
         out[c, pl.ds(rows0, 24), :] = jnp.where(slot24 == 5, roll_lanes(v, -7), v)
 
-    def main_z(v, c, i, j):
-        edge = roll_lanes(inj[c, pl.ds(pl.multiple_of(i * 24, 8) + G, 24), :], 123 - 16 * j)
-        up = roll_lanes(jnp.where(lane24 == 0, edge, v), 127)
-        down = roll_lanes(jnp.where(lane24 == 127, edge, v), 1)
+    def make_edges(comps, first, last):
+        def plane(i, j):
+            for c in comps:
+                v = inj[c, pl.ds(pl.multiple_of(i * 24, 8) + G, 24), :]
+                edge[c, pl.ds(row_of(i, j), 24), :] = roll_lanes(v, 123 - 16 * j)
+        for_planes(first, last, plane)
+
+    def main_z(v, c, b):
+        e = edge[c, pl.ds(b, 24), :]
+        up = roll_lanes(jnp.where(lane24 == 0, e, v), 127)
+        down = roll_lanes(jnp.where(lane24 == 127, e, v), 1)
         return up, down
 
     def slab_x(v, below, above):
@@ -268,7 +275,7 @@
             for j in range(8):
                 body(i, j)
             return 0
-        lax.fori_loop(1, 4, block, 0)
+        lax.fori_loop(1, 4, block, 0, unroll=3)
         for p in range(32, last + 1):
             body(4, p - 32)
 
@@ -322,13 +329,14 @@
             inj[0, pl.ds(base, 24), :] = jnp.where(slot24 == 5, roll_lanes(v, -7), v)
             return 0
         lax.fori_loop(0, 5, injection, 0)
+        make_edges((0,), 0, 39)
 
         def main_block(i, _):
             fives = roll_rows(jnp.where(sub8 < 4, r5[pl.ds(pl.multiple_of(i * 8, 8) + 8, 8), :], r5[pl.ds(pl.multiple_of(i * 8, 8), 8), :]), 4)
             for j in range(8):
                 b = row_of(i, j)
                 e = ext[pl.ds(b, 24), :]
-                up, down = main_z(e, 0, i, j)
+                up, down = main_z(e, 0, b)
                 five = jnp.broadcast_to(fives[j:j + 1, :], (24, 128))
                 below = jnp.where(sub24 == 0, five, ext[pl.ds(b - 1, 24), :])
                 nbrs = (
@@ -384,12 +392,12 @@
             inj[0, pl.ds(b, 24), :] = jnp.where(slot24 == 5, roll_lanes(p, -7), p)
             return 0
         lax.fori_loop(0, 5, slab_block, 0)
+        make_edges((0,), 0, 38)
 
         def plane(i, j):
             b = row_of(i, j)
             p = ext[pl.ds(b, 24), :]
-            edge = roll_lanes(inj[0, pl.ds(pl.multiple_of(i * 24, 8) + G, 24), :], 123 - 16 * j)
-            zu = roll_lanes(jnp.where(lane24 == 0, edge, p), 127)
+            zu = roll_lanes(jnp.where(lane24 == 0, edge[0, pl.ds(b, 24), :], p), 127)
             nbrs = (ext[pl.ds(b + 24, 24), :], ext[pl.ds(b + 1, 24), :], zu)
             for c in range(3):
                 smain[c, pl.ds(b, 24), :] = wmain[c, pl.ds(b, 24), :] * (nbrs[c] - p)
@@ -419,13 +427,14 @@
 
     def sweep(src, dst, ssrc, sdst, first, last, with_slab):
         injections(ssrc)
+        make_edges((0, 1, 2), first, last)
 
         def plane(i, j):
             b = row_of(i, j)
             k = [kmain[f, pl.ds(b, 24), :] for f in range(6)]
             for c in range(3):
                 v = src[c, pl.ds(b, 24), :]
-                zu, zd = main_z(v, c, i, j)
+                zu, zd = main_z(v, c, b)
                 total = k[0] * src[c, pl.ds(b - 24, 24), :] + k[1] * src[c, pl.ds(b + 24, 24), :]
                 total = total + (k[2] * shift_rows(src, c, b, -1) + k[3] * shift_rows(src, c, b, 1))
                 total = total + (k[4] * zd + k[5] * zu)
@@ -455,12 +464,12 @@
             make_injection(ssrc, 2, b, inj)
             return 0
         lax.fori_loop(0, 5, block, 0, unroll=True)
+        make_edges((2,), 4, 35)
 
         def plane(i, j):
             b = row_of(i, j) + 4
             x, y, z = (src[c, pl.ds(b, 16), :] for c in range(3))
-            edge = roll_lanes(inj[2, pl.ds(pl.multiple_of(i * 24, 8) + (G + 4), 16), :], 123 - 16 * j)
-            zd = roll_lanes(jnp.where(iota((16, 128), 1) == 127, edge, z), 1)
+            zd = roll_lanes(jnp.where(iota((16, 128), 1) == 127, edge[2, pl.ds(b, 16), :], z), 1)
             total = (src[0, pl.ds(b - 24, 16), :] - x) + (src[1, pl.ds(b - 1, 16), :] - y) + (zd - z)
             to = pl.multiple_of(i * 128, 16) + (j * 16 - 64)
             out[pl.ds(to, 16), :] = total
@@ -766,7 +775,7 @@
             v((3, EROWS, 128), F32), v((3, SROWS, 128), F32),
             v((3, EROWS, 128), F32), v((3, EROWS, 128), F32),
             v((3, SROWS, 128), F32), v((3, SROWS, 128), F32),
-            v((3, SROWS, 128), F32),
+            v((3, SROWS, 128), F32), v((3, EROWS, 128), F32),
             *[v((ROWS, 128), F32) for _ in range(7)],
             v((ITERS, 8, 128), F32), v((ITERS, nz, 8, 128), F32), v((ITERS, nx * ny, 8, 128), F32),
             dma((2,)), dma((2,)), dma((NSETS, 26)), dma((NSETS, 26)), dma, dma,

time: 122 us -> 82.8 us (0.68)
  Pallas kernels: 117 us -> 78.4 us
    pallas_call x1, Pallas kernels: 117 us -> 78.4 us  [per_device(): pl.pallas_call(functools.partial(kernel, sizes), out_shape=(jax.ShapeDtyp...]
where the time goes in v1:
time: 82.8 us; the launch traced here: 82.6 us
  Pallas kernels  78.4 us (95%)
  local copies, waits for them, and re-layouts  3.61 us (4%)
    pallas_call x1, Pallas kernels, per_device(): pl.pallas_call(functools.partial(kernel, sizes), out_shape=(jax.ShapeDtyp...  78.4 us
    unnamed x4, local copies, waits for them, and re-layouts  2.42 us

profile of v1, /device:TPU:1, one launch (start us, length us, event | category | flops | bytes accessed | tf_op | source)
XLA Modules:
  0.0 82.6 jit_solution(12935878791038604341)
XLA Ops:
  0.6 78.4 %shard_map.67 = (f32[512,128]{1,0:T(8,128)}, f32[512,128]{1,0:T(8,128)}, f32[8,128]{1,0:T(8,128)}) custom-call(f32[3,512,128]{2,1,0:T(8,128)} %bitcast.6, s32[512,128]{1,0:T(8,128)} %bitcast.7, f32[8]{0:T(128)} %table.1, s32[6]{0:T(128)} %flags.1), custom_call_target="tpu_custom_call" | custom-call | tf_op jit(solution)/shard_map/pallas_call | solution.py:786
  79.0 1.2 %slice_bitcast_fusion = f32[3]{0:T(128)} fusion(f32[8,128]{1,0:T(8,128)} %get-tuple-element.8), kind=kLoop, calls=%fused_computation | loop fusion | bytes 24 | tf_op jit(solution)/shard_map/squeeze | solution.py:800
  80.2 0.0 copy-start
  80.2 1.7 %copy.9 = f32[32,16,128]{2,1,0:T(8,128)} copy(f32[32,16,128]{2,1,0:T(8,128)} %bitcast.9) | data formatting | bytes 524288
  81.9 0.0 copy-done
  81.9 0.7 copy.10
Async XLA Ops:
  80.2 1.7 %copy-start = (f32[512,128]{1,0:T(8,128)S(1)}, f32[512,128]{1,0:T(8,128)}, u32[]{:S(2)}) copy-start(f32[512,128]{1,0:T(8,128)} %get-tuple-element.7) | copy-start | bytes 786436

commit v2 on v0

v2 whole, which is shorter than its diff:
```python
import functools

import jax
import jax.numpy as jnp
from jax import lax
from jax.experimental import pallas as pl
from jax.experimental.pallas import tpu as pltpu
from jax.sharding import PartitionSpec as P

ITERS = 3
OMEGA = 0.8
F32 = jnp.float32
MESH = pl.DeviceIdType.MESH

BX, BY, BZ = 32, 16, 128
ROWS = BX * BY
PLANES = 53
EROWS = PLANES * 24
NSETS = 7

DIRS = [(dx, dy, dz) for dz in (0, 1, -1) for dy in (1, -1, 0) for dx in (0, 1, -1) if (dx, dy, dz) != (0, 0, 0)]
DIRS.sort(key=lambda d: (d[1] == 0 or d[0] != 0 or d[2] != 0, sum(map(abs, d))))
DIR_AT = {d: i for i, d in enumerate(DIRS)}


def piece_rows(d):
    dx, dy, dz = d
    if dz == 0:
        if dx and dy:
            return 16
        return 128 if dy else 80
    if dx and dy:
        return 8
    if dy:
        return 32
    return 16 if dx else 64


OFFSETS = {}
RECV_ROWS = 0
for _d in DIRS:
    OFFSETS[_d] = RECV_ROWS
    RECV_ROWS += piece_rows(_d)


def iota(shape, dim):
    return lax.broadcasted_iota(jnp.int32, shape, dim)


def roll_lanes(v, by):
    by = by % 128
    return v if by == 0 else pltpu.roll(v, by, 1)


def roll_rows(v, by):
    return pltpu.roll(v, by % v.shape[0], 0)


def kernel(
    sizes,
    force_hbm, phase_hbm, table, flags,
    press_out, resid_out, norms_out,
    phase, field, ystage, cstage, dstage, y5, recv, r5, f5,
    ext, faces, weights, source, va, vb, halo, dslab,
    res, sch, wap, sim, tim, nap, pre,
    red, red1, red2, scal, norm,
    in_sem, send_sem, recv_sem, send5_sem, recv5_sem, rs1, rr1, rs2, rr2,
):
    nx, ny, nz = sizes
    at = (lax.axis_index("gx"), lax.axis_index("gy"), lax.axis_index("gz"))

    def neighbour(d):
        ok = None
        for dim in range(3):
            if d[dim] == 0:
                continue
            here = at[dim] < sizes[dim] - 1 if d[dim] > 0 else at[dim] > 0
            ok = here if ok is None else jnp.logical_and(ok, here)
        return ok, tuple(at[dim] + d[dim] for dim in range(3))

    def recv_at(k, d, start=0, rows=None):
        return recv.at[k, pl.ds(OFFSETS[d] + start, piece_rows(d) if rows is None else rows)]

    def pieces(k, d):
        dx, dy, dz = d
        to = tuple(-a for a in d)
        if dz == 0:
            if dx and dy:
                side = 0 if dy < 0 else 1
                src = ystage.at[k, side, pl.ds(0 if dx < 0 else 112, 16)]
                return src, recv_at(k, to)
            if dy:
                return ystage.at[k, 0 if dy < 0 else 1], recv_at(k, to)
            if dx < 0:
                return field.at[k, pl.ds(0, 64)], recv_at(k, to, 0, 64)
            return field.at[k, pl.ds(ROWS - 80, 80)], recv_at(k, to)
        if dx and dy:
            return dstage.at[k, pl.ds(0 if dx < 0 else 24, 8)], recv_at(k, to)
        if dy:
            return dstage.at[k], recv_at(k, to)
        if dx:
            return cstage.at[k, pl.ds(0 if dx < 0 else 48, 16)], recv_at(k, to)
        return cstage.at[k], recv_at(k, to)

    def copy_of(k, d):
        src, dst = pieces(k, d)
        _, device = neighbour(d)
        to = tuple(-a for a in d)
        return pltpu.make_async_remote_copy(
            src_ref=src, dst_ref=dst,
            send_sem=send_sem.at[k, DIR_AT[d]], recv_sem=recv_sem.at[k, DIR_AT[to]],
            device_id=device, device_id_type=MESH,
        )

    def incoming(k, d):
        to = tuple(-a for a in d)
        src, dst = pieces(k, to)
        return pltpu.make_async_remote_copy(
            src_ref=src, dst_ref=dst,
            send_sem=send_sem.at[k, DIR_AT[to]], recv_sem=recv_sem.at[k, DIR_AT[d]],
            device_id=at, device_id_type=MESH,
        )

    sub8 = iota((8, 128), 0)
    lane8 = iota((8, 128), 1)
    group8, slot8 = lane8 // 16, lane8 % 16
    lane24 = iota((24, 128), 1)
    sub24 = iota((24, 128), 0)
    group24, slot24 = lane24 // 32, lane24 % 32
    bigroup8, bislot8 = lane8 // 32, lane8 % 32


    def pack_y(k):
        def pair(xp, _):
            base = pl.multiple_of(xp * 32, 32)
            a0, a1 = field[k, pl.ds(base, 8), :], field[k, pl.ds(base + 8, 8), :]
            b0, b1 = field[k, pl.ds(base + 16, 8), :], field[k, pl.ds(base + 24, 8), :]
            to = pl.multiple_of(xp * 8, 8)
            ystage[k, 0, pl.ds(to, 8), :] = jnp.where(sub8 < 4, a0, roll_rows(b0, 4))
            ystage[k, 1, pl.ds(to, 8), :] = jnp.where(sub8 < 4, roll_rows(a1, 4), b1)
            return 0
        lax.fori_loop(0, BX // 2, pair, 0, unroll=16)

    def pack_z(k):
        def block(xb, _):
            acc = [[jnp.zeros((8, 128), F32) for _ in range(2)] for _ in range(3)]
            for g in range(8):
                base = pl.multiple_of(xb * 128, 128) + g * 16
                a, b = field[k, pl.ds(base, 8), :], field[k, pl.ds(base + 8, 8), :]
                for i, v in enumerate((a, b, jnp.where(sub8 < 4, a, b))):
                    acc[i][0] = jnp.where(group8 == g, roll_lanes(v, 16 * g), acc[i][0])
                    acc[i][1] = jnp.where(group8 == g, roll_lanes(v, 9 + 16 * g), acc[i][1])
            a, b, c = (jnp.where(slot8 < 4, u, v) for u, v in acc)
            to = pl.multiple_of(xb * 16, 16)
            cstage[k, pl.ds(to, 8), :] = a
            cstage[k, pl.ds(to + 8, 8), :] = b
            dstage[k, pl.ds(pl.multiple_of(xb * 8, 8), 8), :] = c
            return 0
        lax.fori_loop(0, 4, block, 0, unroll=4)

    flat = [d for d in DIRS if d[2] == 0]
    deep = [d for d in DIRS if d[2] != 0]

    def send(k, dirs):
        for d in dirs:
            ok, _ = neighbour(d)

            @pl.when(ok)
            def _():
                copy_of(k, d).start()

    def exchange_start(k):
        pack_y(k)
        send(k, flat)
        pack_z(k)
        send(k, deep)

    def receive(k, dirs):
        for d in dirs:
            ok, _ = neighbour(d)

            @pl.when(ok)
            def _():
                incoming(k, d).wait_recv()

    def finish_sends(k):
        for d in DIRS:
            ok, _ = neighbour(d)

            @pl.when(ok)
            def _():
                copy_of(k, d).wait_send()

    def main_row(x):
        return (1 + x) * 24

    def slab_row(l):
        return (42 + l) * 24

    def refresh(ref):
        low, high = pl.ds(slab_row(9), 24), pl.ds(slab_row(0), 24)
        ref[pl.ds(slab_row(-1), 24), :] = roll_lanes(ref[low, :], 32)
        ref[pl.ds(slab_row(10), 24), :] = roll_lanes(ref[high, :], -32)

    def unpack(k):
        receive(k, flat)

        def planes(own, low, high, first, pairs):
            for xp in range(pairs):
                lo, hi = low(xp * 8), high(xp * 8)
                los, his = roll_rows(lo, 4), roll_rows(hi, 4)
                for half in range(2):
                    ra, rb = (roll_rows(own(xp * 32 + 16 * half + 8 * t), 4) for t in range(2))
                    to = main_row(first + 2 * xp + half)
                    ext[pl.ds(to, 8), :] = jnp.where(sub8 < 4, (lo, los)[half], ra)
                    ext[pl.ds(to + 8, 8), :] = jnp.where(sub8 < 4, ra, rb)
                    ext[pl.ds(to + 16, 8), :] = jnp.where(sub8 < 4, rb, (his, hi)[half])

        def of(d, start=0):
            return lambda row: recv[k, pl.ds(row + (OFFSETS[d] + start), 8), :]

        planes(lambda r: field[k, pl.ds(r, 8), :], of((0, -1, 0)), of((0, 1, 0)), 4, 16)
        planes(of((-1, 0, 0), 16), of((-1, -1, 0)), of((-1, 1, 0)), 0, 2)
        planes(of((1, 0, 0)), of((1, -1, 0)), of((1, 1, 0)), 36, 2)

        def own(i, _):
            for u in range(5):
                for t in range(3):
                    lo, hi = None, None
                    for h in range(4):
                        v = ext[pl.ds(pl.multiple_of(i * 120, 8) + (main_row(10 * h + u) + 8 * t), 8), :]
                        a, b = roll_lanes(v, 32 * h + 9), roll_lanes(v, 32 * h + 18)
                        lo = a if h == 0 else jnp.where(bigroup8 == h, a, lo)
                        hi = b if h == 0 else jnp.where(bigroup8 == h, b, hi)
                    to = pl.ds(pl.multiple_of(i * 120, 8) + (slab_row(u) + 8 * t), 8)
                    ext[to, :] = jnp.where(bislot8 < 9, lo, hi)
            return 0
        lax.fori_loop(0, 2, own, 0)
        receive(k, deep)

        def merged(d, row):
            low = recv[k, pl.ds(OFFSETS[(d[0], d[1], -1)] + row, 8), :]
            high = recv[k, pl.ds(OFFSETS[(d[0], d[1], 1)] + row, 8), :]
            return jnp.where(slot8 < 4, high, low)

        inner = []
        for t in range(2):
            inner.append([merged((-1, 0), 8 * t)] + [merged((0, 0), xb * 16 + 8 * t) for xb in range(4)] + [merged((1, 0), 8 * t)])
        sides = []
        for xb in range(6):
            dx, row = (-1, 0) if xb == 0 else (1, 0) if xb == 5 else (0, (xb - 1) * 8)
            sides.append(roll_rows(jnp.where(sub8 < 4, merged((dx, 1), row), merged((dx, -1), row)), 4))

        def shifted(parts, i):
            return roll_lanes(jnp.where(group8 < 4, parts[i + 1], parts[i]), 64)

        def arrived(_, carry):
            for i in range(5):
                a, b = roll_rows(shifted(inner[0], i), 4), roll_rows(shifted(inner[1], i), 4)
                c = shifted(sides, i)
                tiles = (jnp.where(sub8 < 4, c, a), jnp.where(sub8 < 4, a, b), jnp.where(sub8 < 4, b, c))
                for t in range(3):
                    halo[pl.ds(i * 24 + 8 * t, 8), :] = tiles[t]
            return carry
        lax.fori_loop(0, 1, arrived, 0)

        def outer(l, _):
            for t in range(3):
                acc = None
                for h in range(4):
                    x = 10 * h + l
                    v = halo[pl.ds(x // 8 * 24 + 8 * t, 8), :]
                    a = roll_lanes(v, 32 * h + 9 - 16 * (x % 8))
                    acc = a if h == 0 else jnp.where(bigroup8 == h, a, acc)
                to = pl.ds(slab_row(l) + 8 * t, 8)
                ext[to, :] = jnp.where((bislot8 >= 9) & (bislot8 < 18), acc, ext[to, :])
            return 0
        for l in range(10):
            outer(l, 0)


    walls = [jnp.where(flags[f] == 0, F32(1.0), F32(0.0)) for f in range(6)]
    totals = (nx * BX, ny * BY, nz * BZ)

    def coefficients(b, e, nbrs, spots):
        inside = None
        diag = jnp.zeros_like(e)
        extra = [jnp.zeros_like(e) for _ in range(3)]
        for axis in range(3):
            for side in range(2):
                spot = spots[axis] + (1 if side else -1)
                here = (spot >= 0) & (spot < totals[axis])
                face = 0.5 * (e + nbrs[axis][side])
                wall = walls[2 * axis + side]
                outer = jnp.where(here, F32(0.0), e)
                diag = diag + jnp.where(here, face, e * wall)
                extra[axis] = extra[axis] + outer * (1.0 - wall)
                faces[2 * axis + side, pl.ds(b, 24), :] = face
            here = (spots[axis] >= 0) & (spots[axis] < totals[axis])
            inside = here if inside is None else inside & here
        for c in range(3):
            d = diag + extra[c]
            good = inside & (d > 0)
            weights[c, pl.ds(b, 24), :] = jnp.where(good, OMEGA / jnp.where(good, d, F32(1.0)), F32(0.0))

    def setup():
        keep = None
        for t in range(2):
            v = roll_rows(recv[0, pl.ds(OFFSETS[(-1, 0, 0)] + 8 * t, 8), :], 4)
            if t == 0:
                ext[pl.ds(0, 8), :] = jnp.where(sub8 < 4, F32(0.0), v)
                keep = v
            else:
                ext[pl.ds(8, 8), :] = jnp.where(sub8 < 4, keep, v)
                ext[pl.ds(16, 8), :] = jnp.where(sub8 < 4, v, F32(0.0))
        first = ext[pl.ds(0, 24), :]
        first = jnp.where(slot24 < 9, roll_lanes(first, 9), roll_lanes(first, 18))
        low = pl.ds(slab_row(-1), 24)
        ext[low, :] = jnp.where(group24 == 0, first, ext[low, :])
        five = None
        lane16 = iota((16, 128), 1)
        for h in range(4):
            v = r5[pl.ds(10 * h + 4, 16), :]
            v = jnp.where(lane16 % 32 < 9, roll_lanes(v, 32 * h + 9), roll_lanes(v, 32 * h + 18))
            five = v if h == 0 else jnp.where(lane16 // 32 == h, v, five)
        f5[...] = five

        def neighbours(b, below):
            e = ext[pl.ds(b, 24), :]
            return e, (
                (ext[pl.ds(b - 24, 24), :], ext[pl.ds(b + 24, 24), :]),
                (jnp.where(sub24 == 0, below, ext[pl.ds(b - 1, 24), :]), ext[pl.ds(b + 1, 24), :]),
                (roll_lanes(e, 1), roll_lanes(e, 127)),
            )

        ys = sub24 + (at[1] * BY - 4)

        def main_block(i, _):
            fives = roll_rows(jnp.where(sub8 < 4, r5[pl.ds(pl.multiple_of(i * 8, 8) + 8, 8), :], r5[pl.ds(pl.multiple_of(i * 8, 8), 8), :]), 4)
            for j in range(8):
                b = pl.multiple_of(i * 192, 8) + main_row(j)
                e, nbrs = neighbours(b, jnp.broadcast_to(fives[j:j + 1, :], (24, 128)))
                coefficients(b, e, nbrs, (
                    jnp.broadcast_to(at[0] * BX + (i * 8 + j - 4), (24, 128)), ys, lane24 + at[2] * BZ,
                ))
            return 0
        lax.fori_loop(0, 5, main_block, 0)
        zs = jnp.where(slot24 < 13, slot24 + 119, slot24 - 18) + at[2] * BZ

        for l in range(10):
            b = slab_row(l)
            e, nbrs = neighbours(b, jnp.broadcast_to(f5[l:l + 1, :], (24, 128)))
            coefficients(b, e, nbrs, (group24 * 10 + (at[0] * BX - 4 + l), ys, zs))


    SLAB = [slab_row(l) for l in range(10)]

    def gradient():
        for b in SLAB + [main_row(x) for x in range(39)]:
            p = ext[pl.ds(b, 24), :]
            nbrs = (ext[pl.ds(b + 24, 24), :], ext[pl.ds(b + 1, 24), :], roll_lanes(p, 127))
            for c in range(3):
                source[c, pl.ds(b, 24), :] = weights[c, pl.ds(b, 24), :] * (nbrs[c] - p)

    def scaled_force(c):
        def block(i, _):
            for u in range(13):
                b = pl.multiple_of(i * 312, 8) + 24 * (u + 1)
                source[c, pl.ds(b, 24), :] = weights[c, pl.ds(b, 24), :] * ext[pl.ds(b, 24), :]
            return 0
        lax.fori_loop(0, 4, block, 0)

    def ends(ref):
        def each(c, _):
            refresh(ref.at[c])
            return 0
        lax.fori_loop(0, 3, each, 0, unroll=3)

    def sweep(src, dst, first, last):
        for b in SLAB + [main_row(x) for x in range(first, last + 1)]:
            k = [faces[f, pl.ds(b, 24), :] for f in range(6)]
            for c in range(3):
                v = src[c, pl.ds(b, 24), :]
                total = k[0] * src[c, pl.ds(b - 24, 24), :] + k[1] * src[c, pl.ds(b + 24, 24), :]
                total = total + (k[2] * src[c, pl.ds(b - 1, 24), :] + k[3] * src[c, pl.ds(b + 1, 24), :])
                total = total + (k[4] * roll_lanes(v, 1) + k[5] * roll_lanes(v, 127))
                dst[c, pl.ds(b, 24), :] = (
                    (1.0 - OMEGA) * v + source[c, pl.ds(b, 24), :] + weights[c, pl.ds(b, 24), :] * total
                )
        ends(dst)

    def minus_divergence(src, b, rows):
        x, y, z = (src[c, pl.ds(b, rows), :] for c in range(3))
        return (src[0, pl.ds(b - 24, rows), :] - x) + (src[1, pl.ds(b - 1, rows), :] - y) + (roll_lanes(z, 1) - z)

    def divergence(src, out):
        def slab_part(i, _):
            for u in range(5):
                b = pl.multiple_of(i * 120, 8) + slab_row(u)
                dslab[pl.ds(pl.multiple_of(i * 120, 8) + u * 24, 24), :] = minus_divergence(src, b, 24)
            return 0
        lax.fori_loop(0, 2, slab_part, 0)

        def together(i, _):
            for u in range(5):
                b = pl.ds(pl.multiple_of(i * 120, 8) + u * 24, 24)
                v = dslab[b, :]
                dslab[b, :] = jnp.where(slot24 < 9, v, roll_lanes(v, -9))
            return 0
        lax.fori_loop(0, 2, together, 0)
        lane16 = iota((16, 128), 1)
        for x in range(4, 36):
            h, l = divmod(x, 10)
            total = minus_divergence(src, main_row(x) + 4, 16)
            edge = roll_lanes(dslab[pl.ds(l * 24 + 4, 16), :], -(9 + 32 * h))
            out[pl.ds((x - 4) * 16, 16), :] = jnp.where((lane16 < 8) | (lane16 >= 124), edge, total)

    def apply(out):
        ends(source)
        sweep(source, va, 1, 37)
        sweep(va, vb, 2, 36)
        sweep(vb, va, 3, 35)
        divergence(va, out)


    me_z = at[2]
    me_xy = at[0] * ny + at[1]
    nxy = nx * ny

    def z_copy(k, off):
        other = lax.rem(me_z + off, nz)
        return pltpu.make_async_remote_copy(
            src_ref=red.at[k], dst_ref=red1.at[k, me_z], send_sem=rs1.at[k, off], recv_sem=rr1.at[k, off],
            device_id=(at[0], at[1], other), device_id_type=MESH,
        )

    def xy_copy(k, ox, oy):
        off = ox * ny + oy
        return pltpu.make_async_remote_copy(
            src_ref=red.at[k], dst_ref=red2.at[k, me_xy], send_sem=rs2.at[k, off], recv_sem=rr2.at[k, off],
            device_id=(lax.rem(at[0] + ox, nx), lax.rem(at[1] + oy, ny), at[2]), device_id_type=MESH,
        )

    offsets_xy = [(ox, oy) for ox in range(nx) for oy in range(ny) if (ox, oy) != (0, 0)]

    def reduce_start(k):
        red1[k, me_z] = red[k]
        for off in range(1, nz):
            z_copy(k, off).start()

    def reduce_middle(k):
        for off in range(1, nz):
            z_copy(k, off).wait_recv()
        for off in range(1, nz):
            z_copy(k, off).wait_send()
        value = red1[k, 0]
        for i in range(1, nz):
            value = value + red1[k, i]
        red[k] = value
        red2[k, me_xy] = value
        for ox, oy in offsets_xy:
            xy_copy(k, ox, oy).start()

    cells = float(totals[0] * totals[1] * totals[2])

    def reduce_end(k):
        for ox, oy in offsets_xy:
            xy_copy(k, ox, oy).wait_recv()
        for ox, oy in offsets_xy:
            xy_copy(k, ox, oy).wait_send()
        value = red2[k, 0]
        for i in range(1, nxy):
            value = value + red2[k, i]
        value = jnp.broadcast_to(jnp.sum(value, axis=1, keepdims=True), (8, 128))
        gamma, delta, squares = (jnp.broadcast_to(value[i:i + 1, :], (8, 128)) for i in range(3))
        norm[k] = squares / cells
        gamma_old, alpha_old = scal[0], scal[1]
        if isinstance(k, int):
            beta = gamma / gamma_old
            alpha = gamma / (delta - beta * gamma / alpha_old)
        else:
            beta = jnp.where(k == 0, F32(0.0), gamma / gamma_old)
            alpha = gamma / (delta - jnp.where(k == 0, F32(0.0), beta * gamma / alpha_old))
        scal[0] = gamma
        scal[1] = alpha
        return alpha, beta


    load_phase = pltpu.make_async_copy(phase_hbm, phase, in_sem.at[0])
    load_force = pltpu.make_async_copy(force_hbm, field.at[pl.ds(1, 3)], in_sem.at[1])
    load_phase.start()
    load_force.start()

    def clear_recv(i, _):
        for k in range(NSETS):
            recv[k, pl.ds(pl.multiple_of(i * 8, 8), 8), :] = jnp.zeros((8, 128), F32)
        return 0
    lax.fori_loop(0, RECV_ROWS // 8, clear_recv, 0, unroll=2)

    for t in range(0, 56, 8):
        r5[pl.ds(t, 8), :] = jnp.zeros((8, 128), F32)

    barrier = pltpu.get_barrier_semaphore()
    count = jnp.int32(0)
    for d in DIRS:
        ok, device = neighbour(d)

        @pl.when(ok)
        def _():
            pl.semaphore_signal(barrier, inc=1, device_id=device, device_id_type=MESH)
        count = count + ok.astype(jnp.int32)
    for off in range(1, nz):
        pl.semaphore_signal(barrier, inc=1, device_id=(at[0], at[1], lax.rem(me_z + off, nz)), device_id_type=MESH)
    for ox, oy in offsets_xy:
        pl.semaphore_signal(
            barrier, inc=1, device_id=(lax.rem(at[0] + ox, nx), lax.rem(at[1] + oy, ny), at[2]), device_id_type=MESH
        )
    count = count + (nz - 1 + nxy - 1)

    zero24 = jnp.zeros((24, 128), F32)
    ext[pl.ds(0, 24), :] = zero24
    for ref in (source, va, vb):
        for c in range(3):
            for plane in (0, 1, 2, 3, 38, 39, 40, 41, 52):
                ref[c, pl.ds(plane * 24, 24), :] = zero24
    for f in range(6):
        faces[f, pl.ds(41 * 24, 24), :] = zero24
    for c in range(3):
        weights[c, pl.ds(41 * 24, 24), :] = zero24
        weights[c, pl.ds(52 * 24, 24), :] = zero24
    zero8 = jnp.zeros((8, 128), F32)
    scal[0] = zero8 + 1.0
    scal[1] = zero8 + 1.0
    for ref in (sch, sim, tim, pre):
        def clear(i, _):
            ref[pl.ds(pl.multiple_of(i * 64, 64), 64), :] = jnp.zeros((64, 128), F32)
            return 0
        lax.fori_loop(0, ROWS // 64, clear, 0)

    load_phase.wait()

    def lookup(i, _):
        for u in range(4):
            r = pl.multiple_of(i * 32, 32) + 8 * u
            ids = phase[pl.ds(r, 8), :]
            eta = jnp.zeros((8, 128), F32)
            for level in range(8):
                eta = eta + jnp.where(ids == level, table[level], F32(0.0))
            field[0, pl.ds(r, 8), :] = eta
        return 0
    lax.fori_loop(0, ROWS // 32, lookup, 0)
    for x in range(BX):
        y5[pl.ds(x, 1), :] = field[0, pl.ds(x * 16 + 11, 1), :]
    pl.semaphore_wait(barrier, count)
    has_y_up, _ = neighbour((0, 1, 0))
    has_y_down, _ = neighbour((0, -1, 0))
    copy5_out = pltpu.make_async_remote_copy(
        src_ref=y5, dst_ref=r5.at[pl.ds(8, 32)], send_sem=send5_sem, recv_sem=recv5_sem,
        device_id=(at[0], at[1] + 1, at[2]), device_id_type=MESH,
    )

    @pl.when(has_y_up)
    def _():
        copy5_out.start()

    def send_first(k, _):
        @pl.when(k == 1)
        def _():
            load_force.wait()
        exchange_start(k)
        return 0
    lax.fori_loop(0, 4, send_first, 0)

    def rows_loop(body, init, step=8):
        def block(i, carry):
            for u in range(step):
                carry = body(pl.ds(pl.multiple_of(i * (8 * step), 8 * step) + 8 * u, 8), carry)
            return carry
        return lax.fori_loop(0, ROWS // (8 * step), block, init)

    def partials(sums):
        sums = [jnp.broadcast_to(jnp.sum(v, axis=0, keepdims=True), (8, 128)) for v in sums]
        return jnp.where(sub8 == 0, sums[0], jnp.where(sub8 == 1, sums[1], jnp.where(sub8 == 2, sums[2], F32(0.0))))

    def advance(alpha, beta, last):
        def step(at_r, carry):
            e, rr, w, n = field[0, at_r, :], res[at_r, :], wap[at_r, :], nap[at_r, :]
            p = e * rr + beta * sch[at_r, :]
            s = w + beta * sim[at_r, :]
            t = n + beta * tim[at_r, :]
            sch[at_r, :] = p
            sim[at_r, :] = s
            tim[at_r, :] = t
            pre[at_r, :] = pre[at_r, :] + alpha * p
            rr = rr - alpha * s
            w = w - alpha * t
            res[at_r, :] = rr
            wap[at_r, :] = w
            field[last, at_r, :] = e * w
            return carry[0] + rr * (e * rr), carry[1] + w * (e * rr), carry[2] + rr * rr
        return partials(rows_loop(step, (zero8, zero8, zero8)))

    def stage(k, _):
        unpack(k)

        @pl.when(k == 0)
        def _():
            @pl.when(has_y_down)
            def _():
                copy5_out.wait_recv()
            refresh(ext)
            setup()

        @pl.when((k >= 1) & (k < 4))
        def _():
            scaled_force(k - 1)

        @pl.when(k >= 5)
        def _():
            reduce_middle(k - 5)

        @pl.when(k >= 4)
        def _():
            refresh(ext)
            gradient()

        @pl.when(k >= 3)
        def _():
            apply(nap)

        @pl.when(k == 3)
        def _():
            def step(at_r, _):
                r = nap[at_r, :]
                res[at_r, :] = r
                field[4, at_r, :] = field[0, at_r, :] * r
                return 0
            rows_loop(step, 0)

        @pl.when(k == 4)
        def _():
            def step(at_r, carry):
                e, rr, w = field[0, at_r, :], res[at_r, :], nap[at_r, :]
                z = e * rr
                wap[at_r, :] = w
                field[5, at_r, :] = e * w
                return carry[0] + rr * z, carry[1] + w * z, carry[2] + rr * rr
            red[0] = partials(rows_loop(step, (zero8, zero8, zero8)))

        @pl.when(k >= 5)
        def _():
            alpha, beta = reduce_end(k - 5)
            red[k - 4] = advance(alpha, beta, k + 1)

        @pl.when((k >= 3) & (k < 6))
        def _():
            exchange_start(k + 1)

        @pl.when(k >= 4)
        def _():
            reduce_start(k - 4)
        return 0
    lax.fori_loop(0, NSETS, stage, 0)

    reduce_middle(2)
    alpha, beta = reduce_end(2)

    def step2(at_r, _):
        rr = res[at_r, :]
        p = field[0, at_r, :] * rr + beta * sch[at_r, :]
        s = wap[at_r, :] + beta * sim[at_r, :]
        press_out[at_r, :] = pre[at_r, :] + alpha * p
        resid_out[at_r, :] = rr - alpha * s
        return 0
    rows_loop(step2, 0)
    norms_out[...] = jnp.where(lane8 == 0, norm[0], jnp.where(lane8 == 1, norm[1], norm[2]))

    def finish(k, _):
        finish_sends(k)
        return 0
    lax.fori_loop(0, NSETS, finish, 0)

    @pl.when(has_y_up)
    def _():
        copy5_out.wait_send()


def solution(mesh):
    sizes = (mesh.shape["gx"], mesh.shape["gy"], mesh.shape["gz"])
    nx, ny, nz = sizes

    def per_device(force, phase, table, flags):
        v = functools.partial(pltpu.VMEM)
        dma = pltpu.SemaphoreType.DMA
        scratch = [
            v((ROWS, 128), jnp.int32),
            v((NSETS + 1, ROWS, 128), F32),
            v((NSETS, 2, 128, 128), F32),
            v((NSETS, 64, 128), F32),
            v((NSETS, 32, 128), F32),
            v((32, 128), F32),
            v((NSETS, RECV_ROWS, 128), F32),
            v((56, 128), F32), v((16, 128), F32),
            v((EROWS, 128), F32),
            v((6, EROWS, 128), F32), v((3, EROWS, 128), F32), v((3, EROWS, 128), F32),
            v((3, EROWS, 128), F32), v((3, EROWS, 128), F32),
            v((120, 128), F32), v((240, 128), F32),
            *[v((ROWS, 128), F32) for _ in range(7)],
            v((ITERS, 8, 128), F32), v((ITERS, nz, 8, 128), F32), v((ITERS, nx * ny, 8, 128), F32),
            v((2, 8, 128), F32), v((ITERS, 8, 128), F32),
            dma((2,)), dma((NSETS, 26)), dma((NSETS, 26)), dma, dma,
            dma((ITERS, nz)), dma((ITERS, nz)), dma((ITERS, nx * ny)), dma((ITERS, nx * ny)),
        ]
        hbm = pl.BlockSpec(memory_space=pl.ANY)
        smem = pl.BlockSpec(memory_space=pltpu.SMEM)
        press, resid, norms = pl.pallas_call(
            functools.partial(kernel, sizes),
            out_shape=(
                pltpu.VMEM((ROWS, 128), F32),
                pltpu.VMEM((ROWS, 128), F32),
                jax.ShapeDtypeStruct((8, 128), F32),
            ),
            in_specs=[hbm, hbm, smem, smem],
            out_specs=(pl.BlockSpec(memory_space=pltpu.VMEM), pl.BlockSpec(memory_space=pltpu.VMEM), pl.BlockSpec(memory_space=pltpu.VMEM)),
            scratch_shapes=scratch,
            compiler_params=pltpu.CompilerParams(
                collective_id=0, has_side_effects=True, vmem_limit_bytes=60 * 1024 * 1024
            ),
        )(force.reshape(3, ROWS, BZ), phase.reshape(ROWS, BZ), table, flags)
        return press.reshape(BX, BY, BZ), resid.reshape(BX, BY, BZ), norms[0, :ITERS]

    return jax.shard_map(
        per_device,
        mesh=mesh,
        in_specs=(P(None, "gx", "gy", "gz"), P("gx", "gy", "gz"), P(), P()),
        out_specs=(P("gx", "gy", "gz"), P("gx", "gy", "gz"), P()),
        check_vma=False,
    )
```

time: 122 us -> 73.1 us (0.60)
  Pallas kernels: 117 us -> 69.7 us
    pallas_call x1, Pallas kernels: 117 us -> 69.7 us  [per_device(): pl.pallas_call(functools.partial(kernel, sizes), out_shape=(pltpu.VMEM((R...]
where the time goes in v2:
time: 73.1 us; the launch traced here: 72.9 us
  Pallas kernels  69.7 us (95%)
  local copies, waits for them, and re-layouts  2.59 us (4%)
    pallas_call x1, Pallas kernels, per_device(): pl.pallas_call(functools.partial(kernel, sizes), out_shape=(pltpu.VMEM((R...  69.7 us

profile of v2, /device:TPU:1, one launch (start us, length us, event | category | flops | bytes accessed | tf_op | source)
XLA Modules:
  0.0 72.9 jit_solution(16837805510583859533)
XLA Ops:
  0.6 69.7 %shard_map.67 = (f32[512,128]{1,0:T(8,128)S(1)}, f32[512,128]{1,0:T(8,128)S(1)}, f32[8,128]{1,0:T(8,128)}) custom-call(f32[3,512,128]{2,1,0:T(8,128)} %bitcast.8, s32[512,128]{1,0:T(8,128)} %bitcast.9, f32[8]{0:T(128)} %table.1, s32[6]{0:T(128)} %flags.1), custom_call_target="tpu_custom_call" | custom-call | tf_op jit(solution)/shard_map/pallas_call | solution.py:716
  70.3 0.7 copy.9
  71.0 0.7 copy.10
  71.7 1.2 %slice_bitcast_fusion = f32[3]{0:T(128)} fusion(f32[8,128]{1,0:T(8,128)} %get-tuple-element.8), kind=kLoop, calls=%fused_computation | loop fusion | bytes 24 | tf_op jit(solution)/shard_map/squeeze | solution.py:730

commit v3 on v2

--- a/solution.py
+++ b/solution.py
@@ -32,7 +32,7 @@
     if dx and dy:
         return 8
     if dy:
-        return 32
+        return 16
     return 16 if dx else 64
 
 
@@ -63,7 +63,7 @@
     phase, field, ystage, cstage, dstage, y5, recv, r5, f5,
     ext, faces, weights, source, va, vb, halo, dslab,
     res, sch, wap, sim, tim, nap, pre,
-    red, red1, red2, scal, norm,
+    red, total1, red1, red2, scal, norm,
     in_sem, send_sem, recv_sem, send5_sem, recv5_sem, rs1, rr1, rs2, rr2,
 ):
     nx, ny, nz = sizes
@@ -94,10 +94,11 @@
             if dx < 0:
                 return field.at[k, pl.ds(0, 64)], recv_at(k, to, 0, 64)
             return field.at[k, pl.ds(ROWS - 80, 80)], recv_at(k, to)
+        side = 0 if dy < 0 else 1
         if dx and dy:
-            return dstage.at[k, pl.ds(0 if dx < 0 else 24, 8)], recv_at(k, to)
+            return dstage.at[k, side, pl.ds(0 if dx < 0 else 8, 8)], recv_at(k, to)
         if dy:
-            return dstage.at[k], recv_at(k, to)
+            return dstage.at[k, side], recv_at(k, to)
         if dx:
             return cstage.at[k, pl.ds(0 if dx < 0 else 48, 16)], recv_at(k, to)
         return cstage.at[k], recv_at(k, to)
@@ -142,21 +143,27 @@
         lax.fori_loop(0, BX // 2, pair, 0, unroll=16)
 
     def pack_z(k):
-        def block(xb, _):
-            acc = [[jnp.zeros((8, 128), F32) for _ in range(2)] for _ in range(3)]
-            for g in range(8):
-                base = pl.multiple_of(xb * 128, 128) + g * 16
-                a, b = field[k, pl.ds(base, 8), :], field[k, pl.ds(base + 8, 8), :]
-                for i, v in enumerate((a, b, jnp.where(sub8 < 4, a, b))):
-                    acc[i][0] = jnp.where(group8 == g, roll_lanes(v, 16 * g), acc[i][0])
-                    acc[i][1] = jnp.where(group8 == g, roll_lanes(v, 9 + 16 * g), acc[i][1])
-            a, b, c = (jnp.where(slot8 < 4, u, v) for u, v in acc)
-            to = pl.multiple_of(xb * 16, 16)
-            cstage[k, pl.ds(to, 8), :] = a
-            cstage[k, pl.ds(to + 8, 8), :] = b
-            dstage[k, pl.ds(pl.multiple_of(xb * 8, 8), 8), :] = c
-            return 0
-        lax.fori_loop(0, 4, block, 0, unroll=4)
+        def block(xp, _):
+            ends = []
+            for u in range(2):
+                acc = [[None, None] for _ in range(3)]
+                for g in range(8):
+                    base = pl.multiple_of(xp * 256, 256) + (u * 128 + g * 16)
+                    a, b = field[k, pl.ds(base, 8), :], field[k, pl.ds(base + 8, 8), :]
+                    for i, v in enumerate((a, b, jnp.where(sub8 < 4, a, b))):
+                        for m in range(2):
+                            r = roll_lanes(v, 9 * m + 16 * g)
+                            acc[i][m] = r if g == 0 else jnp.where(group8 == g, r, acc[i][m])
+                a, b, c = (jnp.where(slot8 < 4, lo, hi) for lo, hi in acc)
+                to = pl.multiple_of(xp * 32, 32) + u * 16
+                cstage[k, pl.ds(to, 8), :] = a
+                cstage[k, pl.ds(to + 8, 8), :] = b
+                ends.append(c)
+            to = pl.ds(pl.multiple_of(xp * 8, 8), 8)
+            dstage[k, 0, to, :] = jnp.where(sub8 < 4, ends[0], roll_rows(ends[1], 4))
+            dstage[k, 1, to, :] = jnp.where(sub8 < 4, roll_rows(ends[0], 4), ends[1])
+            return 0
+        lax.fori_loop(0, 2, block, 0, unroll=2)
 
     flat = [d for d in DIRS if d[2] == 0]
     deep = [d for d in DIRS if d[2] != 0]
@@ -174,6 +181,14 @@
         send(k, flat)
         pack_z(k)
         send(k, deep)
+
+    def pack_first(k, _):
+        @pl.when(k == 1)
+        def _():
+            load_force.wait()
+        pack_y(k)
+        pack_z(k)
+        return 0
 
     def receive(k, dirs):
         for d in dirs:
@@ -248,8 +263,12 @@
             inner.append([merged((-1, 0), 8 * t)] + [merged((0, 0), xb * 16 + 8 * t) for xb in range(4)] + [merged((1, 0), 8 * t)])
         sides = []
         for xb in range(6):
-            dx, row = (-1, 0) if xb == 0 else (1, 0) if xb == 5 else (0, (xb - 1) * 8)
-            sides.append(roll_rows(jnp.where(sub8 < 4, merged((dx, 1), row), merged((dx, -1), row)), 4))
+            dx, row = (-1, 0) if xb == 0 else (1, 0) if xb == 5 else (0, (xb - 1) // 2 * 8)
+            above, below = merged((dx, 1), row), merged((dx, -1), row)
+            if xb % 2 == 1:
+                sides.append(jnp.where(sub8 < 4, below, roll_rows(above, 4)))
+            else:
+                sides.append(jnp.where(sub8 < 4, roll_rows(below, 4), above))
 
         def shifted(parts, i):
             return roll_lanes(jnp.where(group8 < 4, parts[i + 1], parts[i]), 64)
@@ -428,17 +447,22 @@
     nxy = nx * ny
 
     def z_copy(k, off):
-        other = lax.rem(me_z + off, nz)
         return pltpu.make_async_remote_copy(
-            src_ref=red.at[k], dst_ref=red1.at[k, me_z], send_sem=rs1.at[k, off], recv_sem=rr1.at[k, off],
-            device_id=(at[0], at[1], other), device_id_type=MESH,
+            src_ref=red.at[k], dst_ref=red1.at[k, me_z], send_sem=rs1.at[k], recv_sem=rr1.at[k],
+            device_id=(at[0], at[1], lax.rem(me_z + off, nz)), device_id_type=MESH,
         )
 
     def xy_copy(k, ox, oy):
-        off = ox * ny + oy
         return pltpu.make_async_remote_copy(
-            src_ref=red.at[k], dst_ref=red2.at[k, me_xy], send_sem=rs2.at[k, off], recv_sem=rr2.at[k, off],
+            src_ref=total1.at[k], dst_ref=red2.at[k, me_xy], send_sem=rs2.at[k], recv_sem=rr2.at[k],
             device_id=(lax.rem(at[0] + ox, nx), lax.rem(at[1] + oy, ny), at[2]), device_id_type=MESH,
+        )
+
+    def all_of(k, ref, count, sent, arrived):
+        part = ref.at[k, pl.ds(0, count)]
+        return pltpu.make_async_remote_copy(
+            src_ref=part, dst_ref=part, send_sem=sent.at[k], recv_sem=arrived.at[k],
+            device_id=at, device_id_type=MESH,
         )
 
     offsets_xy = [(ox, oy) for ox in range(nx) for oy in range(ny) if (ox, oy) != (0, 0)]
@@ -449,14 +473,11 @@
             z_copy(k, off).start()
 
     def reduce_middle(k):
-        for off in range(1, nz):
-            z_copy(k, off).wait_recv()
-        for off in range(1, nz):
-            z_copy(k, off).wait_send()
+        all_of(k, red1, nz - 1, rs1, rr1).wait_recv()
         value = red1[k, 0]
         for i in range(1, nz):
             value = value + red1[k, i]
-        red[k] = value
+        total1[k] = value
         red2[k, me_xy] = value
         for ox, oy in offsets_xy:
             xy_copy(k, ox, oy).start()
@@ -464,15 +485,13 @@
     cells = float(totals[0] * totals[1] * totals[2])
 
     def reduce_end(k):
-        for ox, oy in offsets_xy:
-            xy_copy(k, ox, oy).wait_recv()
-        for ox, oy in offsets_xy:
-            xy_copy(k, ox, oy).wait_send()
+        all_of(k, red2, nxy - 1, rs2, rr2).wait_recv()
         value = red2[k, 0]
         for i in range(1, nxy):
             value = value + red2[k, i]
-        value = jnp.broadcast_to(jnp.sum(value, axis=1, keepdims=True), (8, 128))
-        gamma, delta, squares = (jnp.broadcast_to(value[i:i + 1, :], (8, 128)) for i in range(3))
+        gamma, delta, squares = (
+            jnp.broadcast_to(jnp.sum(value[i], axis=1, keepdims=True), (8, 128)) for i in range(3)
+        )
         norm[k] = squares / cells
         gamma_old, alpha_old = scal[0], scal[1]
         if isinstance(k, int):
@@ -551,6 +570,7 @@
     lax.fori_loop(0, ROWS // 32, lookup, 0)
     for x in range(BX):
         y5[pl.ds(x, 1), :] = field[0, pl.ds(x * 16 + 11, 1), :]
+    lax.fori_loop(0, 4, pack_first, 0)
     pl.semaphore_wait(barrier, count)
     has_y_up, _ = neighbour((0, 1, 0))
     has_y_down, _ = neighbour((0, -1, 0))
@@ -564,10 +584,8 @@
         copy5_out.start()
 
     def send_first(k, _):
-        @pl.when(k == 1)
-        def _():
-            load_force.wait()
-        exchange_start(k)
+        send(k, flat)
+        send(k, deep)
         return 0
     lax.fori_loop(0, 4, send_first, 0)
 
@@ -578,9 +596,9 @@
             return carry
         return lax.fori_loop(0, ROWS // (8 * step), block, init)
 
-    def partials(sums):
-        sums = [jnp.broadcast_to(jnp.sum(v, axis=0, keepdims=True), (8, 128)) for v in sums]
-        return jnp.where(sub8 == 0, sums[0], jnp.where(sub8 == 1, sums[1], jnp.where(sub8 == 2, sums[2], F32(0.0))))
+    def keep_partials(k, sums):
+        for i in range(3):
+            red[k, i] = jnp.sum(sums[i], axis=0, keepdims=True)
 
     def advance(alpha, beta, last):
         def step(at_r, carry):
@@ -598,7 +616,7 @@
             wap[at_r, :] = w
             field[last, at_r, :] = e * w
             return carry[0] + rr * (e * rr), carry[1] + w * (e * rr), carry[2] + rr * rr
-        return partials(rows_loop(step, (zero8, zero8, zero8)))
+        return rows_loop(step, (zero8, zero8, zero8))
 
     def stage(k, _):
         unpack(k)
@@ -645,12 +663,12 @@
                 wap[at_r, :] = w
                 field[5, at_r, :] = e * w
                 return carry[0] + rr * z, carry[1] + w * z, carry[2] + rr * rr
-            red[0] = partials(rows_loop(step, (zero8, zero8, zero8)))
+            keep_partials(0, rows_loop(step, (zero8, zero8, zero8)))
 
         @pl.when(k >= 5)
         def _():
             alpha, beta = reduce_end(k - 5)
-            red[k - 4] = advance(alpha, beta, k + 1)
+            keep_partials(k - 4, advance(alpha, beta, k + 1))
 
         @pl.when((k >= 3) & (k < 6))
         def _():
@@ -677,6 +695,11 @@
 
     def finish(k, _):
         finish_sends(k)
+
+        @pl.when(k < ITERS)
+        def _():
+            all_of(k, red1, nz - 1, rs1, rr1).wait_send()
+            all_of(k, red2, nxy - 1, rs2, rr2).wait_send()
         return 0
     lax.fori_loop(0, NSETS, finish, 0)
 
@@ -697,7 +720,7 @@
             v((NSETS + 1, ROWS, 128), F32),
             v((NSETS, 2, 128, 128), F32),
             v((NSETS, 64, 128), F32),
-            v((NSETS, 32, 128), F32),
+            v((NSETS, 2, 16, 128), F32),
             v((32, 128), F32),
             v((NSETS, RECV_ROWS, 128), F32),
             v((56, 128), F32), v((16, 128), F32),
@@ -706,10 +729,11 @@
             v((3, EROWS, 128), F32), v((3, EROWS, 128), F32),
             v((120, 128), F32), v((240, 128), F32),
             *[v((ROWS, 128), F32) for _ in range(7)],
-            v((ITERS, 8, 128), F32), v((ITERS, nz, 8, 128), F32), v((ITERS, nx * ny, 8, 128), F32),
+            v((ITERS, 3, 1, 128), F32), v((ITERS, 3, 1, 128), F32),
+            v((ITERS, nz, 3, 1, 128), F32), v((ITERS, nx * ny, 3, 1, 128), F32),
             v((2, 8, 128), F32), v((ITERS, 8, 128), F32),
             dma((2,)), dma((NSETS, 26)), dma((NSETS, 26)), dma, dma,
-            dma((ITERS, nz)), dma((ITERS, nz)), dma((ITERS, nx * ny)), dma((ITERS, nx * ny)),
+            dma((ITERS,)), dma((ITERS,)), dma((ITERS,)), dma((ITERS,)),
         ]
         hbm = pl.BlockSpec(memory_space=pl.ANY)
         smem = pl.BlockSpec(memory_space=pltpu.SMEM)

time: 73.1 us -> 69.5 us (0.951)
  Pallas kernels: 69.7 us -> 66.1 us
    pallas_call x1, Pallas kernels: 69.7 us -> 66.1 us  [per_device(): pl.pallas_call(functools.partial(kernel, sizes), out_shape=(pltpu.VMEM((R...]
where the time goes in v3:
time: 69.5 us; the launch traced here: 69.4 us
  Pallas kernels  66.1 us (95%)
  local copies, waits for them, and re-layouts  2.59 us (4%)
    pallas_call x1, Pallas kernels, per_device(): pl.pallas_call(functools.partial(kernel, sizes), out_shape=(pltpu.VMEM((R...  66.1 us
    unnamed x2, local copies, waits for them, and re-layouts  1.41 us

profile of v3, /device:TPU:1, one launch (start us, length us, event | category | flops | bytes accessed | tf_op | source)
XLA Modules:
  0.0 69.4 jit_solution(6426536511150004579)
XLA Ops:
  0.6 66.1 %shard_map.67 = (f32[512,128]{1,0:T(8,128)S(1)}, f32[512,128]{1,0:T(8,128)S(1)}, f32[8,128]{1,0:T(8,128)}) custom-call(f32[3,512,128]{2,1,0:T(8,128)} %bitcast.8, s32[512,128]{1,0:T(8,128)} %bitcast.9, f32[8]{0:T(128)} %table.1, s32[6]{0:T(128)} %flags.1), custom_call_target="tpu_custom_call" | custom-call | tf_op jit(solution)/shard_map/pallas_call | solution.py:740
  66.8 0.7 %copy.9 = f32[32,16,128]{2,1,0:T(8,128)} copy(f32[32,16,128]{2,1,0:T(8,128)S(1)} %bitcast.7) | data formatting | bytes 524288
  67.5 0.7 %copy.10 = f32[32,16,128]{2,1,0:T(8,128)} copy(f32[32,16,128]{2,1,0:T(8,128)S(1)} %bitcast.6) | data formatting | bytes 524288
  68.2 1.2 %slice_bitcast_fusion = f32[3]{0:T(128)} fusion(f32[8,128]{1,0:T(8,128)} %get-tuple-element.8), kind=kLoop, calls=%fused_computation | loop fusion | bytes 24 | tf_op jit(solution)/shard_map/squeeze | solution.py:754

commit v4 on v3

--- a/solution.py
+++ b/solution.py
@@ -109,7 +109,7 @@
         to = tuple(-a for a in d)
         return pltpu.make_async_remote_copy(
             src_ref=src, dst_ref=dst,
-            send_sem=send_sem.at[k, DIR_AT[d]], recv_sem=recv_sem.at[k, DIR_AT[to]],
+            send_sem=send_sem.at[DIR_AT[d]], recv_sem=recv_sem.at[lax.rem(k, 5), DIR_AT[to]],
             device_id=device, device_id_type=MESH,
         )
 
@@ -118,7 +118,7 @@
         src, dst = pieces(k, to)
         return pltpu.make_async_remote_copy(
             src_ref=src, dst_ref=dst,
-            send_sem=send_sem.at[k, DIR_AT[to]], recv_sem=recv_sem.at[k, DIR_AT[d]],
+            send_sem=send_sem.at[DIR_AT[to]], recv_sem=recv_sem.at[lax.rem(k, 5), DIR_AT[d]],
             device_id=at, device_id_type=MESH,
         )
 
@@ -198,13 +198,18 @@
             def _():
                 incoming(k, d).wait_recv()
 
-    def finish_sends(k):
+    def finish_sends():
         for d in DIRS:
-            ok, _ = neighbour(d)
+            ok, device = neighbour(d)
+            rows = 64 if d == (-1, 0, 0) else piece_rows(d)
 
             @pl.when(ok)
             def _():
-                copy_of(k, d).wait_send()
+                part = recv.at[pl.ds(0, NSETS), pl.ds(0, rows)]
+                pltpu.make_async_remote_copy(
+                    src_ref=part, dst_ref=part, send_sem=send_sem.at[DIR_AT[d]], recv_sem=recv_sem.at[0, DIR_AT[d]],
+                    device_id=device, device_id_type=MESH,
+                ).wait_send()
 
     def main_row(x):
         return (1 + x) * 24
@@ -217,7 +222,7 @@
         ref[pl.ds(slab_row(-1), 24), :] = roll_lanes(ref[low, :], 32)
         ref[pl.ds(slab_row(10), 24), :] = roll_lanes(ref[high, :], -32)
 
-    def unpack(k):
+    def unpack_flat(k):
         receive(k, flat)
 
         def planes(own, low, high, first, pairs):
@@ -251,6 +256,8 @@
                     ext[to, :] = jnp.where(bislot8 < 9, lo, hi)
             return 0
         lax.fori_loop(0, 2, own, 0)
+
+    def unpack_deep(k):
         receive(k, deep)
 
         def merged(d, row):
@@ -374,20 +381,20 @@
 
     SLAB = [slab_row(l) for l in range(10)]
 
-    def gradient():
-        for b in SLAB + [main_row(x) for x in range(39)]:
+    def gradient(planes):
+        for b in planes:
             p = ext[pl.ds(b, 24), :]
             nbrs = (ext[pl.ds(b + 24, 24), :], ext[pl.ds(b + 1, 24), :], roll_lanes(p, 127))
             for c in range(3):
                 source[c, pl.ds(b, 24), :] = weights[c, pl.ds(b, 24), :] * (nbrs[c] - p)
 
-    def scaled_force(c):
+    def scaled_force(c, first, count):
         def block(i, _):
-            for u in range(13):
-                b = pl.multiple_of(i * 312, 8) + 24 * (u + 1)
+            for u in range(10):
+                b = pl.multiple_of(i * 240, 8) + (first + 24 * u)
                 source[c, pl.ds(b, 24), :] = weights[c, pl.ds(b, 24), :] * ext[pl.ds(b, 24), :]
             return 0
-        lax.fori_loop(0, 4, block, 0)
+        lax.fori_loop(0, count // 10, block, 0)
 
     def ends(ref):
         def each(c, _):
@@ -395,8 +402,8 @@
             return 0
         lax.fori_loop(0, 3, each, 0, unroll=3)
 
-    def sweep(src, dst, first, last):
-        for b in SLAB + [main_row(x) for x in range(first, last + 1)]:
+    def sweep(src, dst, planes):
+        for b in planes:
             k = [faces[f, pl.ds(b, 24), :] for f in range(6)]
             for c in range(3):
                 v = src[c, pl.ds(b, 24), :]
@@ -406,7 +413,6 @@
                 dst[c, pl.ds(b, 24), :] = (
                     (1.0 - OMEGA) * v + source[c, pl.ds(b, 24), :] + weights[c, pl.ds(b, 24), :] * total
                 )
-        ends(dst)
 
     def minus_divergence(src, b, rows):
         x, y, z = (src[c, pl.ds(b, rows), :] for c in range(3))
@@ -434,11 +440,17 @@
             edge = roll_lanes(dslab[pl.ds(l * 24 + 4, 16), :], -(9 + 32 * h))
             out[pl.ds((x - 4) * 16, 16), :] = jnp.where((lane16 < 8) | (lane16 >= 124), edge, total)
 
+    def main_rows(first, last):
+        return [main_row(x) for x in range(first, last + 1)]
+
     def apply(out):
         ends(source)
-        sweep(source, va, 1, 37)
-        sweep(va, vb, 2, 36)
-        sweep(vb, va, 3, 35)
+        sweep(source, va, SLAB)
+        ends(va)
+        sweep(va, vb, SLAB + main_rows(2, 36))
+        ends(vb)
+        sweep(vb, va, SLAB + main_rows(3, 35))
+        ends(va)
         divergence(va, out)
 
 
@@ -510,12 +522,6 @@
     load_phase.start()
     load_force.start()
 
-    def clear_recv(i, _):
-        for k in range(NSETS):
-            recv[k, pl.ds(pl.multiple_of(i * 8, 8), 8), :] = jnp.zeros((8, 128), F32)
-        return 0
-    lax.fori_loop(0, RECV_ROWS // 8, clear_recv, 0, unroll=2)
-
     for t in range(0, 56, 8):
         r5[pl.ds(t, 8), :] = jnp.zeros((8, 128), F32)
 
@@ -535,6 +541,17 @@
             barrier, inc=1, device_id=(lax.rem(at[0] + ox, nx), lax.rem(at[1] + oy, ny), at[2]), device_id_type=MESH
         )
     count = count + (nz - 1 + nxy - 1)
+
+    for d in DIRS:
+        ok, _ = neighbour(d)
+
+        @pl.when(jnp.logical_not(ok))
+        def _():
+            def clear_recv(k, _):
+                for row in range(0, piece_rows(d), 8):
+                    recv[k, pl.ds(OFFSETS[d] + row, 8), :] = jnp.zeros((8, 128), F32)
+                return 0
+            lax.fori_loop(0, NSETS, clear_recv, 0)
 
     zero24 = jnp.zeros((24, 128), F32)
     ext[pl.ds(0, 24), :] = zero24
@@ -619,7 +636,24 @@
         return rows_loop(step, (zero8, zero8, zero8))
 
     def stage(k, _):
-        unpack(k)
+        unpack_flat(k)
+
+        @pl.when(k >= 5)
+        def _():
+            reduce_middle(k - 5)
+
+        @pl.when((k >= 1) & (k < 4))
+        def _():
+            scaled_force(k - 1, main_row(0), 40)
+
+        @pl.when(k >= 4)
+        def _():
+            gradient(main_rows(0, 38))
+
+        @pl.when(k >= 3)
+        def _():
+            sweep(source, va, main_rows(1, 37))
+        unpack_deep(k)
 
         @pl.when(k == 0)
         def _():
@@ -631,16 +665,12 @@
 
         @pl.when((k >= 1) & (k < 4))
         def _():
-            scaled_force(k - 1)
-
-        @pl.when(k >= 5)
-        def _():
-            reduce_middle(k - 5)
+            scaled_force(k - 1, slab_row(0), 10)
 
         @pl.when(k >= 4)
         def _():
             refresh(ext)
-            gradient()
+            gradient(SLAB)
 
         @pl.when(k >= 3)
         def _():
@@ -681,6 +711,14 @@
     lax.fori_loop(0, NSETS, stage, 0)
 
     reduce_middle(2)
+    finish_sends()
+
+    @pl.when(has_y_up)
+    def _():
+        copy5_out.wait_send()
+    for k in range(ITERS):
+        all_of(k, red1, nz - 1, rs1, rr1).wait_send()
+        all_of(k, red2, nxy - 1, rs2, rr2).wait_send()
     alpha, beta = reduce_end(2)
 
     def step2(at_r, _):
@@ -692,20 +730,6 @@
         return 0
     rows_loop(step2, 0)
     norms_out[...] = jnp.where(lane8 == 0, norm[0], jnp.where(lane8 == 1, norm[1], norm[2]))
-
-    def finish(k, _):
-        finish_sends(k)
-
-        @pl.when(k < ITERS)
-        def _():
-            all_of(k, red1, nz - 1, rs1, rr1).wait_send()
-            all_of(k, red2, nxy - 1, rs2, rr2).wait_send()
-        return 0
-    lax.fori_loop(0, NSETS, finish, 0)
-
-    @pl.when(has_y_up)
-    def _():
-        copy5_out.wait_send()
 
 
 def solution(mesh):
@@ -732,7 +756,7 @@
             v((ITERS, 3, 1, 128), F32), v((ITERS, 3, 1, 128), F32),
             v((ITERS, nz, 3, 1, 128), F32), v((ITERS, nx * ny, 3, 1, 128), F32),
             v((2, 8, 128), F32), v((ITERS, 8, 128), F32),
-            dma((2,)), dma((NSETS, 26)), dma((NSETS, 26)), dma, dma,
+            dma((2,)), dma((26,)), dma((5, 26)), dma, dma,
             dma((ITERS,)), dma((ITERS,)), dma((ITERS,)), dma((ITERS,)),
         ]
         hbm = pl.BlockSpec(memory_space=pl.ANY)
@@ -742,7 +766,7 @@
             out_shape=(
                 pltpu.VMEM((ROWS, 128), F32),
                 pltpu.VMEM((ROWS, 128), F32),
-                jax.ShapeDtypeStruct((8, 128), F32),
+                pltpu.VMEM((8, 128), F32),
             ),
             in_specs=[hbm, hbm, smem, smem],
             out_specs=(pl.BlockSpec(memory_space=pltpu.VMEM), pl.BlockSpec(memory_space=pltpu.VMEM), pl.BlockSpec(memory_space=pltpu.VMEM)),

time: 69.5 us -> 65.1 us (0.937)
  Pallas kernels: 66.1 us -> 62.4 us
    pallas_call x1, Pallas kernels: 66.1 us -> 62.4 us  [per_device(): pl.pallas_call(functools.partial(kernel, sizes), out_shape=(pltpu.VMEM((R...]
where the time goes in v4:
time: 65.1 us; the launch traced here: 64.9 us
  Pallas kernels  62.4 us (96%)
  local copies, waits for them, and re-layouts  1.92 us (3%)
    pallas_call x1, Pallas kernels, per_device(): pl.pallas_call(functools.partial(kernel, sizes), out_shape=(pltpu.VMEM((R...  62.4 us
    unnamed x2, local copies, waits for them, and re-layouts  1.41 us

profile of v4, /device:TPU:1, one launch (start us, length us, event | category | flops | bytes accessed | tf_op | source)
XLA Modules:
  0.0 64.9 jit_solution(7262710130174779170)
XLA Ops:
  0.6 62.4 %shard_map.67 = (f32[512,128]{1,0:T(8,128)S(1)}, f32[512,128]{1,0:T(8,128)S(1)}, f32[8,128]{1,0:T(8,128)S(1)}) custom-call(f32[3,512,128]{2,1,0:T(8,128)} %bitcast.8, s32[512,128]{1,0:T(8,128)} %bitcast.9, f32[8]{0:T(128)} %table.1, s32[6]{0:T(128)} %flags.1), custom_call_target="tpu_custom_call" | custom-call | tf_op jit(solution)/shard_map/pallas_call | solution.py:764
  63.0 0.7 %copy.9 = f32[32,16,128]{2,1,0:T(8,128)} copy(f32[32,16,128]{2,1,0:T(8,128)S(1)} %bitcast.7) | data formatting | bytes 524288
  63.7 0.7 %copy.10 = f32[32,16,128]{2,1,0:T(8,128)} copy(f32[32,16,128]{2,1,0:T(8,128)S(1)} %bitcast.6) | data formatting | bytes 524288
  64.4 0.5 slice_bitcast_fusion

commit v5 on v4

--- a/solution.py
+++ b/solution.py
@@ -19,7 +19,7 @@
 NSETS = 7
 
 DIRS = [(dx, dy, dz) for dz in (0, 1, -1) for dy in (1, -1, 0) for dx in (0, 1, -1) if (dx, dy, dz) != (0, 0, 0)]
-DIRS.sort(key=lambda d: (d[1] == 0 or d[0] != 0 or d[2] != 0, sum(map(abs, d))))
+DIRS.sort(key=lambda d: -sum(map(abs, d)))
 DIR_AT = {d: i for i, d in enumerate(DIRS)}
 
 
@@ -255,7 +255,7 @@
                     to = pl.ds(pl.multiple_of(i * 120, 8) + (slab_row(u) + 8 * t), 8)
                     ext[to, :] = jnp.where(bislot8 < 9, lo, hi)
             return 0
-        lax.fori_loop(0, 2, own, 0)
+        lax.fori_loop(0, 2, own, 0, unroll=2)
 
     def unpack_deep(k):
         receive(k, deep)
@@ -379,7 +379,7 @@
             coefficients(b, e, nbrs, (group24 * 10 + (at[0] * BX - 4 + l), ys, zs))
 
 
-    SLAB = [slab_row(l) for l in range(10)]
+    SLAB = [slab_row(l) for l in (9, 0, 1, 2, 3, 4, 5, 6, 7, 8)]
 
     def gradient(planes):
         for b in planes:
@@ -424,7 +424,7 @@
                 b = pl.multiple_of(i * 120, 8) + slab_row(u)
                 dslab[pl.ds(pl.multiple_of(i * 120, 8) + u * 24, 24), :] = minus_divergence(src, b, 24)
             return 0
-        lax.fori_loop(0, 2, slab_part, 0)
+        lax.fori_loop(0, 2, slab_part, 0, unroll=2)
 
         def together(i, _):
             for u in range(5):
@@ -432,7 +432,7 @@
                 v = dslab[b, :]
                 dslab[b, :] = jnp.where(slot24 < 9, v, roll_lanes(v, -9))
             return 0
-        lax.fori_loop(0, 2, together, 0)
+        lax.fori_loop(0, 2, together, 0, unroll=2)
         lane16 = iota((16, 128), 1)
         for x in range(4, 36):
             h, l = divmod(x, 10)

time: 65.1 us -> 63.3 us (0.972)
  Pallas kernels: 62.4 us -> 60.7 us
    pallas_call x1, Pallas kernels: 62.4 us -> 60.7 us  [per_device(): pl.pallas_call(functools.partial(kernel, sizes), out_shape=(pltpu.VMEM((R...]
where the time goes in v5:
time: 63.3 us; the launch traced here: 63.2 us
  Pallas kernels  60.7 us (96%)
  local copies, waits for them, and re-layouts  1.92 us (3%)
  between operations  0.64 us (1%)
    pallas_call x1, Pallas kernels, per_device(): pl.pallas_call(functools.partial(kernel, sizes), out_shape=(pltpu.VMEM((R...  60.7 us
    unnamed x2, local copies, waits for them, and re-layouts  1.41 us

profile of v5, /device:TPU:1, one launch (start us, length us, event | category | flops | bytes accessed | tf_op | source)
XLA Modules:
  0.0 63.2 jit_solution(3508187082541624143)
XLA Ops:
  0.6 60.7 %shard_map.67 = (f32[512,128]{1,0:T(8,128)S(1)}, f32[512,128]{1,0:T(8,128)S(1)}, f32[8,128]{1,0:T(8,128)S(1)}) custom-call(f32[3,512,128]{2,1,0:T(8,128)} %bitcast.8, s32[512,128]{1,0:T(8,128)} %bitcast.9, f32[8]{0:T(128)} %table.1, s32[6]{0:T(128)} %flags.1), custom_call_target="tpu_custom_call" | custom-call | tf_op jit(solution)/shard_map/pallas_call | solution.py:764
  61.3 0.7 %copy.9 = f32[32,16,128]{2,1,0:T(8,128)} copy(f32[32,16,128]{2,1,0:T(8,128)S(1)} %bitcast.7) | data formatting | bytes 524288
  62.0 0.7 %copy.10 = f32[32,16,128]{2,1,0:T(8,128)} copy(f32[32,16,128]{2,1,0:T(8,128)S(1)} %bitcast.6) | data formatting | bytes 524288
  62.7 0.5 slice_bitcast_fusion

commit v6 on v5

--- a/solution.py
+++ b/solution.py
@@ -370,7 +370,7 @@
                     jnp.broadcast_to(at[0] * BX + (i * 8 + j - 4), (24, 128)), ys, lane24 + at[2] * BZ,
                 ))
             return 0
-        lax.fori_loop(0, 5, main_block, 0)
+        lax.fori_loop(0, 5, main_block, 0, unroll=5)
         zs = jnp.where(slot24 < 13, slot24 + 119, slot24 - 18) + at[2] * BZ
 
         for l in range(10):
@@ -606,7 +606,7 @@
         return 0
     lax.fori_loop(0, 4, send_first, 0)
 
-    def rows_loop(body, init, step=8):
+    def rows_loop(body, init, step=16):
         def block(i, carry):
             for u in range(step):
                 carry = body(pl.ds(pl.multiple_of(i * (8 * step), 8 * step) + 8 * u, 8), carry)

time: 63.3 us -> 63.2 us (level)
  no operation moved by 1% of the time
where the time goes in v6:
time: 63.2 us; the launch traced here: 63.1 us
  Pallas kernels  60.5 us (96%)
  local copies, waits for them, and re-layouts  1.92 us (3%)
  between operations  0.64 us (1%)
    pallas_call x1, Pallas kernels, per_device(): pl.pallas_call(functools.partial(kernel, sizes), out_shape=(pltpu.VMEM((R...  60.5 us
    unnamed x2, local copies, waits for them, and re-layouts  1.41 us

profile of v6, /device:TPU:1, one launch (start us, length us, event | category | flops | bytes accessed | tf_op | source)
XLA Modules:
  0.0 63.1 jit_solution(16878937235535286887)
XLA Ops:
  0.6 60.5 %shard_map.67 = (f32[512,128]{1,0:T(8,128)S(1)}, f32[512,128]{1,0:T(8,128)S(1)}, f32[8,128]{1,0:T(8,128)S(1)}) custom-call(f32[3,512,128]{2,1,0:T(8,128)} %bitcast.8, s32[512,128]{1,0:T(8,128)} %bitcast.9, f32[8]{0:T(128)} %table.1, s32[6]{0:T(128)} %flags.1), custom_call_target="tpu_custom_call" | custom-call | tf_op jit(solution)/shard_map/pallas_call | solution.py:764
  61.2 0.7 %copy.9 = f32[32,16,128]{2,1,0:T(8,128)} copy(f32[32,16,128]{2,1,0:T(8,128)S(1)} %bitcast.7) | data formatting | bytes 524288
  61.9 0.7 %copy.10 = f32[32,16,128]{2,1,0:T(8,128)} copy(f32[32,16,128]{2,1,0:T(8,128)S(1)} %bitcast.6) | data formatting | bytes 524288
  62.6 0.5 slice_bitcast_fusion
